TPU v7x, 32 devices: a whole 2x2x4 slice. The times are simulated.
32 devices in a mesh: blk: 16 (over z, y, x), slab: 2 (over core).
Axes of the slice: x: 2, y: 2, z: 4, core: 2. Of those that a mesh axis runs over, the one named last changes fastest.
Arguments:
- sinogram: bfloat16 [32, 8, 2048], P('blk', 'slab'), parts along dimension 1, may hold values from -6 to 6
- jitter: bfloat16 [32], P('blk'), may hold values from -0.29882812 to 0.29882812
- shift: int32 [32], replicated, may hold values from -8 to 8
Outputs:
- image: float32 [32, 8, 2048], P('blk', 'slab'), parts along dimension 1
There are 2 independent parts, one for each index of `slab`. A program takes and returns all parts, laid end to end along the dimension named above; an argument that names none is the same for every part. Nothing has to cross between parts.
All inputs are finite; a program needn't handle non-finite values.
Results may differ from a plain program's by a relative error of at most 0.0055.
Values may be sent and summed in bfloat16 or wider, within the bound.
A program may use at most 64 MiB of HBM per device.

v0:
```python
import functools
import math

import jax
import jax.numpy as jnp
import numpy as np
from jax import lax
from jax.experimental import pallas as pl
from jax.experimental.pallas import tpu as pltpu
from jax.sharding import PartitionSpec as P

LANES = 128
SUBS = 8
BLOCK = 256
PLANE = 4
MESH = pl.DeviceIdType.MESH


def ramp_slab(bins):
    span = 2 * bins - BLOCK
    offsets = (
        np.arange(span, dtype=np.int32)[None, :]
        - np.int32(bins - BLOCK)
        - np.arange(BLOCK, dtype=np.int32)[:, None]
    )
    safe = np.where(offsets == 0, 1, offsets).astype(np.float32)
    odd_part = np.where(
        offsets % 2 != 0, np.float32(-1.0) / (np.float32(math.pi**2) * safe * safe), np.float32(0)
    )
    return np.where(offsets == 0, np.float32(0.25), odd_part).astype(jnp.bfloat16)


def kernel(
    width,
    jit_ref,
    shift_ref,
    sino_ref,
    slab_hbm,
    out_ref,
    slab,
    chunks,
    jmsg,
    jall,
    pvec,
    psm,
    tvec,
    tsm,
    fval,
    fdif,
    acc,
    lsem,
    sj,
    rj,
    sz,
    rz,
    sx,
    rx,
    sy,
    ry,
    sd,
    rd,
):
    me = lax.axis_index("blk")
    ang_dev, slices, bins = sino_ref.shape
    rows_dev = out_ref.shape[0]
    angles = width * ang_dev
    nrows = width * rows_dev
    nblocks = bins // LANES
    ntiles = fval.shape[2]
    depth = width // PLANE
    px, py = me % 2, (me // 2) % 2
    xpeer = me + 1 - 2 * px
    ypeer = me + 2 - 4 * py
    diag = me + 1 - 2 * px + 2 - 4 * py

    def remote(src, dst, send, recv, dev):
        return pltpu.make_async_remote_copy(
            src_ref=src,
            dst_ref=dst,
            send_sem=send,
            recv_sem=recv,
            device_id={"blk": dev},
            device_id_type=MESH,
        )

    def at(dev, k):
        return (dev + width - PLANE * k) % width

    def zcopy(k):
        return remote(
            chunks.at[me], chunks.at[me], sz.at[k], rz.at[k], (me + PLANE * k) % width
        )

    def xcopy(k):
        c = at(me, k)
        return remote(chunks.at[c], chunks.at[c], sx.at[k], rx.at[k], xpeer)

    def ycopy(k):
        c = at(me, k)
        return remote(chunks.at[c], chunks.at[c], sy.at[k], ry.at[k], ypeer)

    def relay_x(k):
        c = at(xpeer, k)
        return remote(
            chunks.at[c, 0], chunks.at[c, 0], sd.at[0, k], rd.at[0, k], ypeer
        )

    def relay_y(k):
        c = at(ypeer, k)
        return remote(
            chunks.at[c, 1], chunks.at[c, 1], sd.at[1, k], rd.at[1, k], xpeer
        )

    def jcopy(i):
        return remote(jmsg, jall.at[me], sj.at[i], rj.at[i], (me + i) % width)

    def relay(k):
        xcopy(k).wait_recv()
        relay_x(k).start()
        ycopy(k).wait_recv()
        relay_y(k).start()

    barrier = pltpu.get_barrier_semaphore()

    @pl.loop(1, width)
    def _(i):
        pl.semaphore_signal(
            barrier, inc=1, device_id={"blk": (me + i) % width}, device_id_type=MESH
        )

    load = pltpu.make_async_copy(slab_hbm, slab, lsem.at[0])
    load.start()

    lane = lax.broadcasted_iota(jnp.int32, (SUBS, LANES), 1)
    sub = lax.broadcasted_iota(jnp.int32, (SUBS, LANES), 0)
    lanef = lane.astype(jnp.float32)
    mine = (lane[:1] % angles) - me * ang_dev
    msg = jnp.zeros((1, LANES), jnp.float32)
    for i in range(ang_dev):
        msg = jnp.where(mine == i, jit_ref[0:1, i : i + 1].astype(jnp.float32), msg)
    jmsg[...] = msg
    jall[me] = msg
    zero = jnp.zeros((SUBS, LANES), jnp.float32)
    for i in range(ang_dev):
        for slot in range(fval.shape[0]):
            for t in [0] + list(range(nblocks + 1, ntiles)):
                fval[slot, i, t] = zero
                fdif[slot, i, t] = zero
    for b in range(nblocks):
        acc[b] = zero

    nb = bins // BLOCK
    flat = jnp.concatenate(
        [sino_ref[i].astype(jnp.float32) for i in range(ang_dev)], axis=0
    )
    lhs = jnp.concatenate(
        [flat[:, i * BLOCK : (i + 1) * BLOCK] for i in range(nb)], axis=0
    ).astype(jnp.bfloat16)
    load.wait()
    total = [None] * nb
    for d in range(2 * nb - 1):
        prod = jnp.dot(
            lhs, slab[:, d * BLOCK : (d + 1) * BLOCK], preferred_element_type=jnp.float32
        )
        for i in range(nb):
            j = d - (nb - 1) + i
            if 0 <= j < nb:
                piece = prod[i * SUBS : (i + 1) * SUBS]
                total[j] = piece if total[j] is None else total[j] + piece
    row = jnp.concatenate(total, axis=1)
    quarter = bins // 4
    for h in range(2):
        chunks[me, h] = jnp.concatenate(
            [row[:, (2 * h + q) * quarter : (2 * h + q + 1) * quarter] for q in range(2)], axis=0
        ).astype(jnp.bfloat16)

    pl.semaphore_wait(barrier, width - 1)

    @pl.loop(1, width)
    def _(i):
        jcopy(i).start()

    @pl.loop(1, depth)
    def _(k):
        zcopy(k).start()

    xcopy(0).start()
    ycopy(0).start()

    relay(0)

    @pl.loop(1, depth)
    def _(k):
        zcopy(k).wait_recv()
        xcopy(k).start()
        ycopy(k).start()

    half = (bins - 1) / 2
    first_row = (me * rows_dev).astype(jnp.float32) - (nrows - 1) / 2
    moved = jnp.zeros((SUBS, LANES), jnp.int32)
    for a in range(angles):
        moved = jnp.where(lane == a, shift_ref[a], moved)
    center = half + moved.astype(jnp.float32) + LANES

    @pl.loop(1, width)
    def _(i):
        jcopy(i).wait()

    jit = jall[0]
    for i in range(1, width):
        jit = jit + jall[i]
    jit = jnp.broadcast_to(jit, (SUBS, LANES))
    ahead = pltpu.roll(jit, LANES - 1, 1)
    behind = pltpu.roll(jit, 1, 1)
    weight = (1.0 + (ahead - behind) * 1.5) * (4.0 / math.sqrt(angles))
    theta = ((lane % angles).astype(jnp.float32) + jit) * math.pi / angles
    cosine = jnp.cos(theta)
    sine = jnp.sin(theta)
    least = jnp.minimum(cosine * (LANES - 1), 0.0) + jnp.minimum(
        first_row * sine, (first_row + (rows_dev - 1)) * sine
    )
    for g in range(nblocks // SUBS):
        group = slice(g * SUBS, (g + 1) * SUBS)
        start = ((sub + g * SUBS) * LANES).astype(jnp.float32) - half
        base = start * cosine + center
        low = (base + least - 0.25).astype(jnp.int32) // LANES
        low = jnp.minimum(jnp.maximum(low, 0), ntiles - 2)
        tvec[group] = low
        pvec[group] = base - (low * LANES).astype(jnp.float32)
    pvec[nblocks:] = jnp.where(sub == 0, cosine, jnp.where(sub == 1, sine, weight))
    moves = [
        pltpu.make_async_copy(pvec, psm, lsem.at[1]),
        pltpu.make_async_copy(tvec, tsm, lsem.at[2]),
    ]
    for move in moves:
        move.start()
    for move in moves:
        move.wait()

    rowf = (sub // slices).astype(jnp.float32) + first_row
    low_half = sub < slices

    def spread(chunk, slot):
        after = [None] * ang_dev
        wts = [psm[nblocks + 2, chunk * ang_dev + i] for i in range(ang_dev)]
        for t in range(nblocks - 1, -2, -1):
            if t >= 0:
                h, q, k = t // (nblocks // 2), (t // (nblocks // 4)) % 2, t % (nblocks // 4)
                tile = chunks[
                    chunk, h, q * SUBS : (q + 1) * SUBS, k * LANES : (k + 1) * LANES
                ].astype(jnp.float32)
                turned = pltpu.roll(tile, slices, 0)
                pair = [
                    jnp.where(low_half, tile, turned) * wts[0],
                    jnp.where(low_half, turned, tile) * wts[1],
                ]
            else:
                pair = [zero] * ang_dev
            for i in range(ang_dev):
                rolled = pltpu.roll(pair[i], LANES - 1, 1)
                nxt = zero if after[i] is None else after[i]
                fdif[slot, i, t + 1] = jnp.where(lane == LANES - 1, nxt, rolled) - pair[i]
                if t >= 0:
                    fval[slot, i, t + 1] = pair[i]
                after[i] = rolled

    def add_up(chunk, slot, sums):
        for i in range(ang_dev):
            a = chunk * ang_dev + i
            ramp = lanef * psm[nblocks, a] + rowf * psm[nblocks + 1, a]
            for b in range(nblocks):
                low = tsm[b, a]
                u = ramp + psm[b, a]
                bin_lo = u.astype(jnp.int32)
                frac = u - bin_lo.astype(jnp.float32)
                where = jnp.bitwise_and(bin_lo, LANES - 1)
                first = bin_lo < LANES

                def pick(ref):
                    return jnp.where(
                        first,
                        jnp.take_along_axis(ref[slot, i, low], where, axis=1, mode="promise_in_bounds"),
                        jnp.take_along_axis(
                            ref[slot, i, low + 1], where, axis=1, mode="promise_in_bounds"
                        ),
                    )

                got = pick(fval) + frac * pick(fdif)
                sums[b] = got if sums[b] is None else sums[b] + got

    def project(*group):
        for slot, chunk in enumerate(group):
            spread(chunk, slot)
        sums = [None] * nblocks
        for slot, chunk in enumerate(group):
            add_up(chunk, slot, sums)
        for b in range(nblocks):
            acc[b] += sums[b]

    def corner(k):
        relay_x(k).wait_recv()
        relay_y(k).wait_recv()

    project(me)

    @pl.loop(1, depth)
    def _(k):
        relay(k)
        project(at(me, k), at(xpeer, k - 1), at(ypeer, k - 1))

    corner(0)
    project(at(xpeer, depth - 1), at(ypeer, depth - 1), at(diag, 0))

    @pl.loop(1, depth - 1)
    def _(k):
        corner(k)
        project(at(diag, k))

    corner(depth - 1)
    project(at(diag, depth - 1))

    for b in range(nblocks):
        done = acc[b]
        for r in range(rows_dev):
            out_ref[r, :, b * LANES : (b + 1) * LANES] = done[r * slices : (r + 1) * slices]

    @pl.loop(0, depth)
    def _(k):
        xcopy(k).wait_send()
        ycopy(k).wait_send()
        relay_x(k).wait_send()
        relay_y(k).wait_send()

    @pl.loop(1, depth)
    def _(k):
        zcopy(k).wait_send()


def body(sinogram, jitter, shift):
    width = lax.axis_size("blk")
    ang_dev, slices, bins = sinogram.shape
    angles = shift.shape[0]
    rows_dev = SUBS // slices
    assert ang_dev == 2 and ang_dev * slices == SUBS and LANES % angles == 0
    assert width % PLANE == 0 and bins % (2 * BLOCK) == 0
    depth = width // PLANE
    ntiles = bins // LANES + 3
    vmem = pl.BlockSpec(memory_space=pltpu.VMEM)
    smem = pl.BlockSpec(memory_space=pltpu.SMEM)
    dma = pltpu.SemaphoreType.DMA
    slab = jnp.asarray(ramp_slab(bins))
    return pl.pallas_call(
        functools.partial(kernel, width),
        out_shape=pltpu.VMEM((rows_dev, slices, bins), jnp.float32),
        in_specs=[vmem, smem, vmem, pl.BlockSpec(memory_space=pl.ANY)],
        out_specs=vmem,
        scratch_shapes=[
            pltpu.VMEM(slab.shape, jnp.bfloat16),
            pltpu.VMEM((width, 2, 2 * SUBS, bins // 4), jnp.bfloat16),
            pltpu.VMEM((1, LANES), jnp.float32),
            pltpu.VMEM((width, 1, LANES), jnp.float32),
            pltpu.VMEM((bins // LANES + SUBS, LANES), jnp.float32),
            pltpu.SMEM((bins // LANES + SUBS, LANES), jnp.float32),
            pltpu.VMEM((bins // LANES, LANES), jnp.int32),
            pltpu.SMEM((bins // LANES, LANES), jnp.int32),
            pltpu.VMEM((3, ang_dev, ntiles, SUBS, LANES), jnp.float32),
            pltpu.VMEM((3, ang_dev, ntiles, SUBS, LANES), jnp.float32),
            pltpu.VMEM((bins // LANES, SUBS, LANES), jnp.float32),
            dma((3,)),
            dma((width,)),
            dma((width,)),
            dma((depth,)),
            dma((depth,)),
            dma((depth,)),
            dma((depth,)),
            dma((depth,)),
            dma((depth,)),
            dma((2, depth)),
            dma((2, depth)),
        ],
        compiler_params=pltpu.CompilerParams(collective_id=0, has_side_effects=True),
    )(jitter.reshape(1, ang_dev), shift, sinogram, slab)


def solution(mesh):
    in_specs = (P("blk", "slab", None), P("blk"), P())
    out_specs = P("blk", "slab", None)
    return jax.shard_map(body, mesh=mesh, in_specs=in_specs, out_specs=out_specs, check_vma=False)
```

profile of v0, /device:TPU:0, one launch (start us, length us, event | category | flops | bytes accessed | tf_op | source)
XLA Modules:
  0.0 20.8 jit_solution(3811090773419114417)
XLA Ops:
  0.0 20.1 %shard_map.46 = f32[2,4,2048]{2,1,0:T(4,128)S(1)} custom-call(bf16[1,2]{1,0:T(2,128)(2,1)} %bitcast.1, s32[32]{0:T(128)} %shift_ref.1, bf16[2,4,2048]{2,1,0:T(4,128)(2,1)} %sino_ref.1, bf16[256,3840]{1,0:T(8,128)(2,1)} %constant.2.clone.slab_hbm), custom_call_target="tpu_custom_call" | custom-call | tf_op jit(solution)/shard_map/pallas_call | solution.py:352
  20.2 0.6 %copy.6 = f32[2,4,2048]{2,1,0:T(4,128)} copy(f32[2,4,2048]{2,1,0:T(4,128)S(1)} %shard_map.46) | data formatting | bytes 131072
where the time goes:
time: 21 us; the launch traced here: 20.8 us
  Pallas kernels  20.1 us (96%)
  local copies, waits for them, and re-layouts  0.63 us (3%)
    pallas_call x1, Pallas kernels, body(): pl.pallas_call(functools.partial(kernel, width), out_shape=pltpu.VMEM((ro...  20.1 us
    unnamed x1, local copies, waits for them, and re-layouts  0.63 us

commit v1 on v0

v1 whole, which is shorter than its diff:
```python
import functools
import math

import jax
import jax.numpy as jnp
import numpy as np
from jax import lax
from jax.experimental import pallas as pl
from jax.experimental.pallas import tpu as pltpu
from jax.sharding import PartitionSpec as P

LANES = 128
SUBS = 8
BLOCK = 256
PLANE = 4
STEP = 64
JITTER = 0.29882812
SHIFT = 8
MESH = pl.DeviceIdType.MESH


def ramp_slab(bins):
    nb = bins // BLOCK
    column = np.arange(BLOCK, dtype=np.int32)
    order = np.concatenate([column[0::2], column[1::2]])
    starts = (np.arange(2 * nb - 1, dtype=np.int32) - (nb - 1)) * BLOCK
    cols = (starts[:, None] + order[None, :]).reshape(-1)
    offsets = cols[None, :] - column[:, None]
    safe = np.where(offsets == 0, 1, offsets).astype(np.float32)
    odd_part = np.where(
        offsets % 2 != 0, np.float32(-1.0) / (np.float32(math.pi**2) * safe * safe), np.float32(0)
    )
    return np.where(offsets == 0, np.float32(0.25), odd_part).astype(jnp.bfloat16)


def window_base(width, ang_dev, rows_dev, bins):
    depth = width // PLANE
    angles, nrows = width * ang_dev, width * rows_dev
    nblocks, per = bins // LANES, PLANE * ang_dev
    groups = depth * rows_dev // SUBS
    half = (bins - 1) / 2
    me = np.arange(width)
    z, q = me // PLANE, me % PLANE
    a = z[:, None] * per + np.arange(per)[None, :]
    theta = (a[..., None] + np.linspace(-JITTER, JITTER, 9)) * math.pi / angles
    zs = np.arange(groups)[:, None] * (SUBS // rows_dev) + np.array([0, SUBS // rows_dev - 1])
    rows = (zs[None] * PLANE + q[:, None, None]) * rows_dev + np.array([0, rows_dev - 1])
    y = rows - (nrows - 1) / 2
    x = np.arange(nblocks)[:, None] * LANES + np.array([0, LANES - 1]) - half
    u = (
        x[None, None, :, None, :, None, None] * np.cos(theta)[:, :, None, None, None, None, :]
        + y[:, None, None, :, None, :, None] * np.sin(theta)[:, :, None, None, None, None, :]
        + half
    )
    low = np.floor(u.min(axis=(4, 5, 6)) - 0.25).astype(np.int32)
    high = u.max(axis=(4, 5, 6)) + 0.25
    assert (high - low).max() + STEP < 2 * LANES
    assert low.min() - SHIFT >= -STEP and low.max() + SHIFT < bins + STEP
    return (low + STEP).reshape(width, 1, per * nblocks * groups)


def lane_gather(x, index):
    dims = lax.GatherDimensionNumbers(
        offset_dims=(),
        collapsed_slice_dims=(1,),
        start_index_map=(1,),
        operand_batching_dims=(0,),
        start_indices_batching_dims=(0,),
    )
    return lax.gather(
        x, index[..., None], dims, (1, 1), mode=lax.GatherScatterMode.PROMISE_IN_BOUNDS
    )


def kernel(
    width,
    jit_hbm,
    shift_hbm,
    sino_hbm,
    slab_hbm,
    base_hbm,
    out_ref,
    jit_ref,
    shift_ref,
    sino_ref,
    slab,
    base,
    chunks,
    jmsg,
    jall,
    tab,
    acc,
    fin,
    snd,
    rcv,
    lsem,
    sj,
    rj,
    s1,
    r1,
    s2,
    r2,
):
    me = lax.axis_index("blk")
    ang_dev, slices, bins = sino_ref.shape
    rows_dev = out_ref.shape[0]
    angles = width * ang_dev
    nrows = width * rows_dev
    nblocks = bins // LANES
    nspans = bins // BLOCK
    depth = width // PLANE
    per = PLANE * ang_dev
    groups = acc.shape[0]
    zper = SUBS // rows_dev
    z, q = me // PLANE, me % PLANE
    half = (bins - 1) / 2

    def remote(src, dst, send, recv, dev):
        return pltpu.make_async_remote_copy(
            src_ref=src,
            dst_ref=dst,
            send_sem=send,
            recv_sem=recv,
            device_id={"blk": dev},
            device_id_type=MESH,
        )

    loads = [
        pltpu.make_async_copy(src, dst, lsem.at[i])
        for i, (src, dst) in enumerate(
            [
                (jit_hbm, jit_ref),
                (sino_hbm, sino_ref),
                (slab_hbm, slab),
                (shift_hbm, shift_ref),
                (base_hbm.at[me], base),
            ]
        )
    ]
    for load in loads:
        load.start()

    barrier = pltpu.get_barrier_semaphore()

    @pl.loop(1, width)
    def _(i):
        pl.semaphore_signal(
            barrier, inc=1, device_id={"blk": (me + i) % width}, device_id_type=MESH
        )

    def peer(d):
        qx, qy = q % 2, q // 2
        return z * PLANE + (qx + d % 2) % 2 + 2 * ((qy + d // 2) % 2)

    def jplane(d):
        return remote(jmsg, jall.at[d], sj.at[d - 1], rj.at[d - 1], peer(d))

    def jnext(p):
        return remote(
            jmsg, jall.at[PLANE], sj.at[PLANE - 1 + p], rj.at[PLANE - 1],
            (z + 1) % depth * PLANE + p,
        )

    def jprev(p):
        return remote(
            jmsg, jall.at[PLANE + 1], sj.at[PLANE - 1 + p], rj.at[PLANE],
            (z + depth - 1) % depth * PLANE + p,
        )

    def share(d):
        return remote(chunks.at[q], chunks.at[q], s1.at[d - 1], r1.at[d - 1], peer(d))

    def give(zt):
        return remote(snd.at[zt], rcv.at[z], s2.at[zt], r2.at[z], zt * PLANE + q)

    def take(zs):
        return remote(snd.at[zs], rcv.at[zs], s2.at[zs], r2.at[zs], zs * PLANE + q)

    lane = lax.broadcasted_iota(jnp.int32, (SUBS, LANES), 1)
    sub = lax.broadcasted_iota(jnp.int32, (SUBS, LANES), 0)
    lanef = lane.astype(jnp.float32)
    zero = jnp.zeros((SUBS, LANES), jnp.float32)
    last = tab.shape[1] - 1
    for p in range(2):
        tab[p, last] = zero
    for g in range(groups):
        for s in range(slices):
            for b in range(nblocks):
                acc[g, s, b] = zero

    loads[0].wait()
    mine = (lane[:1] % angles) - me * ang_dev
    msg = jnp.zeros((1, LANES), jnp.float32)
    for i in range(ang_dev):
        msg = jnp.where(mine == i, jit_ref[0:1, i : i + 1].astype(jnp.float32), msg)
    jmsg[...] = msg
    jall[0] = msg

    loads[1].wait()
    flat = jnp.concatenate(
        [sino_ref[i].astype(jnp.float32) for i in range(ang_dev)], axis=0
    )
    lhs = jnp.concatenate(
        [flat[:, i * BLOCK : (i + 1) * BLOCK] for i in range(nspans)], axis=0
    ).astype(jnp.bfloat16)
    loads[2].wait()
    total = [None] * nspans
    for d in range(2 * nspans - 1):
        prod = jnp.dot(
            lhs, slab[:, d * BLOCK : (d + 1) * BLOCK], preferred_element_type=jnp.float32
        )
        for i in range(nspans):
            j = d - (nspans - 1) + i
            if 0 <= j < nspans:
                piece = prod[i * SUBS : (i + 1) * SUBS]
                total[j] = piece if total[j] is None else total[j] + piece
    for t in range(nspans):
        chunks[q, :, t * LANES : (t + 1) * LANES] = jnp.concatenate(
            [total[t][:, :LANES], total[t][:, LANES:]], axis=0
        ).astype(jnp.bfloat16)

    pl.semaphore_wait(barrier, width - 1)

    for d in (3, 1, 2):
        jplane(d).start()

    @pl.when(q == PLANE - 1)
    def _():
        for p in range(PLANE):
            jnext(p).start()

    @pl.when(q == 0)
    def _():
        for p in range(PLANE):
            jprev(p).start()

    for d in (3, 1, 2):
        share(d).start()

    for d in range(1, PLANE):
        jplane(d).wait_recv()
    jnext(0).wait_recv()
    jprev(0).wait_recv()
    loads[3].wait()
    loads[4].wait()

    jit = jall[0]
    for i in range(1, PLANE + 2):
        jit = jit + jall[i]
    jit = jnp.broadcast_to(jit, (SUBS, LANES))
    ahead = pltpu.roll(jit, LANES - 1, 1)
    behind = pltpu.roll(jit, 1, 1)
    weight = (1.0 + (ahead - behind) * 1.5) * (4.0 / math.sqrt(angles))
    theta = ((lane % angles).astype(jnp.float32) + jit) * math.pi / angles
    cosine = jnp.cos(theta) * 0.5
    sine = jnp.sin(theta) * 0.5
    low_half = sub < slices
    low_row = sub < zper
    ypos = []
    for g in range(groups):
        row = ((sub % zper + g * zper) * PLANE + q) * rows_dev + sub // zper
        ypos.append(row.astype(jnp.float32) - (nrows - 1) / 2)

    @pl.loop(0, PLANE)
    def _(d):
        @pl.when(d > 0)
        def _():
            share(d).wait_recv()

        pc = peer(d)
        qc = pc - z * PLANE
        first = pc * ang_dev
        wts = lane_gather(weight, first + jnp.where(low_half, 0, 1))
        tiles = []
        for t in range(nspans):
            both = chunks[qc, :, t * LANES : (t + 1) * LANES].astype(jnp.float32)
            tiles.append((both[:SUBS] * wts, both[SUBS:] * wts))
        for p in range(2):
            for t in range(nspans):
                tab[p, 4 * t + 1] = tiles[t][p]
            for j in range(1, 4):
                cut = LANES - 32 * j
                turned = [pltpu.roll(tiles[t][p], cut, 1) for t in range(nspans)] + [zero]
                for t in range(nspans):
                    tab[p, 4 * t + j + 1] = jnp.where(lane < cut, turned[t], turned[t + 1])
                if j == 3:
                    tab[p, 0] = jnp.where(lane < cut, 0.0, turned[0])

        spans = []
        for i in range(ang_dev):
            pick = jnp.full((SUBS, LANES), first + i, jnp.int32)
            cosb, sinb = lane_gather(cosine, pick), lane_gather(sine, pick)
            spans.append((cosb, [lanef * cosb + ypos[g] * sinb for g in range(groups)]))
        for b in range(nblocks):
            for g in range(groups):
                sums = [None] * slices
                for i in range(ang_dev):
                    moved = shift_ref[first + i]
                    slot = base[0, ((qc * ang_dev + i) * nblocks + b) * groups + g]
                    slot = lax.shift_right_arithmetic(slot + moved, 6)
                    offset = (moved - slot * STEP).astype(jnp.float32) * 0.5
                    cosb, part = spans[i]
                    h = cosb * (b * LANES - half) + part[g] + (offset + (half + STEP) * 0.5)
                    odd = h.astype(jnp.int32)
                    even = (h + 0.5).astype(jnp.int32)
                    frac = jnp.abs(h - even.astype(jnp.float32)) * 2.0
                    evens, odds = [], []
                    for s in range(slices):
                        r = i * slices + s
                        line = jnp.broadcast_to(tab[0, slot, r : r + 1], (SUBS, LANES))
                        evens.append(lane_gather(line, even))
                    for s in range(slices):
                        r = i * slices + s
                        line = jnp.broadcast_to(tab[1, slot, r : r + 1], (SUBS, LANES))
                        odds.append(lane_gather(line, odd))
                    for s in range(slices):
                        got = evens[s] + frac * (odds[s] - evens[s])
                        sums[s] = got if sums[s] is None else sums[s] + got
                for s in range(slices):
                    acc[g, s, b] += sums[s]

    pos = sub % zper
    for g in range(groups):
        for t in range(nblocks // 2):
            out = [[], [], [], []]
            for b in (2 * t, 2 * t + 1):
                v = [acc[g, s, b] for s in range(slices)]
                w = [None] * 4
                for s in range(2):
                    w[s] = jnp.where(pos < 2, v[s], pltpu.roll(v[s + 2], 2, 0))
                    w[s + 2] = jnp.where(pos < 2, pltpu.roll(v[s], SUBS - 2, 0), v[s + 2])
                for s in (0, 2):
                    lo = jnp.where(pos % 2 < 1, w[s], pltpu.roll(w[s + 1], 1, 0))
                    hi = jnp.where(pos % 2 < 1, pltpu.roll(w[s], SUBS - 1, 0), w[s + 1])
                    for n, val in ((s, lo), (s + 1, hi)):
                        fin[g * zper + n, b] = val
                        out[n].append(val)
            for n in range(4):
                snd[g * zper + n, :, t * LANES : (t + 1) * LANES] = jnp.concatenate(
                    out[n], axis=0
                ).astype(jnp.bfloat16)

    @pl.loop(0, depth)
    def _(zt):
        @pl.when(zt != z)
        def _():
            give(zt).start()

    @pl.loop(1, depth)
    def _(k):
        take((z + k) % depth).wait_recv()

    for t in range(nblocks // 2):
        sums = [fin[z, 2 * t], fin[z, 2 * t + 1]]
        for k in range(1, depth):
            both = rcv[(z + k) % depth, :, t * LANES : (t + 1) * LANES].astype(jnp.float32)
            sums = [sums[0] + both[:SUBS], sums[1] + both[SUBS:]]
        for j in range(2):
            b = 2 * t + j
            for r in range(rows_dev):
                out_ref[r, :, b * LANES : (b + 1) * LANES] = sums[j][r * slices : (r + 1) * slices]

    for d in range(1, PLANE):
        jplane(d).wait_send()
        share(d).wait_send()

    @pl.when(q == PLANE - 1)
    def _():
        for p in range(PLANE):
            jnext(p).wait_send()

    @pl.when(q == 0)
    def _():
        for p in range(PLANE):
            jprev(p).wait_send()

    @pl.loop(1, depth)
    def _(k):
        give((z + k) % depth).wait_send()


def body(sinogram, jitter, shift):
    width = lax.axis_size("blk")
    ang_dev, slices, bins = sinogram.shape
    angles = shift.shape[0]
    rows_dev = SUBS // slices
    depth = width // PLANE
    assert ang_dev == 2 and rows_dev == 2 and slices == 4 and LANES % angles == 0
    assert width % (PLANE * 4) == 0 and bins % (2 * BLOCK) == 0
    groups = depth * rows_dev // SUBS
    nblocks = bins // LANES
    anywhere = pl.BlockSpec(memory_space=pl.ANY)
    dma = pltpu.SemaphoreType.DMA
    slab = jnp.asarray(ramp_slab(bins))
    base = jnp.asarray(window_base(width, ang_dev, rows_dev, bins))
    return pl.pallas_call(
        functools.partial(kernel, width),
        out_shape=pltpu.VMEM((rows_dev, slices, bins), jnp.float32),
        in_specs=[anywhere] * 5,
        out_specs=pl.BlockSpec(memory_space=pltpu.VMEM),
        scratch_shapes=[
            pltpu.VMEM((1, ang_dev), jnp.bfloat16),
            pltpu.SMEM((angles,), jnp.int32),
            pltpu.VMEM((ang_dev, slices, bins), jnp.bfloat16),
            pltpu.VMEM(slab.shape, jnp.bfloat16),
            pltpu.SMEM(base.shape[1:], jnp.int32),
            pltpu.VMEM((PLANE, 2 * SUBS, bins // 2), jnp.bfloat16),
            pltpu.VMEM((1, LANES), jnp.float32),
            pltpu.VMEM((PLANE + 2, 1, LANES), jnp.float32),
            pltpu.VMEM((2, bins // STEP + 2, SUBS, LANES), jnp.float32),
            pltpu.VMEM((groups, slices, nblocks, SUBS, LANES), jnp.float32),
            pltpu.VMEM((depth, nblocks, SUBS, LANES), jnp.float32),
            pltpu.VMEM((depth, 2 * SUBS, bins // 2), jnp.bfloat16),
            pltpu.VMEM((depth, 2 * SUBS, bins // 2), jnp.bfloat16),
            dma((5,)),
            dma((2 * PLANE - 1,)),
            dma((PLANE + 1,)),
            dma((PLANE - 1,)),
            dma((PLANE - 1,)),
            dma((depth,)),
            dma((depth,)),
        ],
        compiler_params=pltpu.CompilerParams(collective_id=0, has_side_effects=True),
    )(jitter.reshape(1, ang_dev), shift, sinogram, slab, base)


def solution(mesh):
    in_specs = (P("blk", "slab", None), P("blk"), P())
    out_specs = P("blk", "slab", None)
    return jax.shard_map(body, mesh=mesh, in_specs=in_specs, out_specs=out_specs, check_vma=False)
```

time: 21 us -> 18.5 us (0.88)
  Pallas kernels: 20.1 us -> 17.7 us
    pallas_call x1, Pallas kernels: 20.1 us -> 17.7 us  [body(): pl.pallas_call(functools.partial(kernel, width), out_shape=pltpu.VMEM((ro...]
where the time goes in v1:
time: 18.5 us; the launch traced here: 18.3 us
  Pallas kernels  17.7 us (96%)
  local copies, waits for them, and re-layouts  0.63 us (3%)
    pallas_call x1, Pallas kernels, body(): pl.pallas_call(functools.partial(kernel, width), out_shape=pltpu.VMEM((ro...  17.7 us
    unnamed x1, local copies, waits for them, and re-layouts  0.63 us

profile of v1, /device:TPU:0, one launch (start us, length us, event | category | flops | bytes accessed | tf_op | source)
XLA Modules:
  0.0 18.3 jit_solution(13778925460194682887)
XLA Ops:
  0.0 17.7 %shard_map.55 = f32[2,4,2048]{2,1,0:T(4,128)S(1)} custom-call(bf16[1,2]{1,0:T(2,128)(2,1)} %bitcast.1, s32[32]{0:T(128)} %shift_hbm.1, bf16[2,4,2048]{2,1,0:T(4,128)(2,1)} %sino_hbm.1, bf16[256,3840]{1,0:T(8,128)(2,1)} %constant.4.clone.slab_hbm, s32[16,1,128]{2,1,0:T(1,128)} %constant.5.clone.base_hbm), custom_call_target="tpu_custom_call" | custom-call | tf_op jit(solution)/shard_map/pallas_call | solution.py:396
  17.7 0.6 %copy.7 = f32[2,4,2048]{2,1,0:T(4,128)} copy(f32[2,4,2048]{2,1,0:T(4,128)S(1)} %shard_map.55) | data formatting | bytes 131072

commit v2 on v1

v2 whole, which is shorter than its diff:
```python
import functools
import math

import jax
import jax.numpy as jnp
import numpy as np
from jax import lax
from jax.experimental import pallas as pl
from jax.experimental.pallas import tpu as pltpu
from jax.sharding import PartitionSpec as P

LANES = 128
SUBS = 8
BLOCK = 256
PLANE = 4
STEP = 64
JITTER = 0.29882812
SHIFT = 8
PIECES = 4
PARTS = 2
MESH = pl.DeviceIdType.MESH


def ramp_slab(bins):
    span = bins // 2
    first = -(span - LANES)
    offset = np.arange(first, span, dtype=np.int32)[None, :] - np.arange(LANES, dtype=np.int32)[:, None]
    both = 2 * np.stack([offset, offset - 1]) + 1
    safe = both.astype(np.float32)
    slab = (np.float32(-1.0) / (np.float32(math.pi**2) * safe * safe)).astype(jnp.bfloat16)
    tiles = slab.reshape(2, LANES, -1, LANES)
    return np.ascontiguousarray(tiles.transpose(2, 0, 1, 3))


def window_base(width, ang_dev, rows_dev, bins):
    depth = width // PLANE
    angles, nrows = width * ang_dev, width * rows_dev
    nblocks, per = bins // LANES, PLANE * ang_dev
    groups = depth * rows_dev // SUBS
    half = (bins - 1) / 2
    me = np.arange(width)
    z, q = me // PLANE, me % PLANE
    a = z[:, None] * per + np.arange(per)[None, :]
    theta = (a[..., None] + np.linspace(-JITTER, JITTER, 9)) * math.pi / angles
    zs = np.arange(groups)[:, None] * (SUBS // rows_dev) + np.array([0, SUBS // rows_dev - 1])
    rows = (zs[None] * PLANE + q[:, None, None]) * rows_dev + np.array([0, rows_dev - 1])
    y = rows - (nrows - 1) / 2
    x = np.arange(nblocks)[:, None] * LANES + np.array([0, LANES - 1]) - half
    u = (
        x[None, None, :, None, :, None, None] * np.cos(theta)[:, :, None, None, None, None, :]
        + y[:, None, None, :, None, :, None] * np.sin(theta)[:, :, None, None, None, None, :]
        + half
    )
    low = np.floor(u.min(axis=(4, 5, 6)) - 0.25).astype(np.int32)
    high = u.max(axis=(4, 5, 6)) + 0.25
    assert (high - low).max() + STEP < 2 * LANES
    assert low.min() - SHIFT >= -STEP and low.max() + SHIFT < bins + STEP
    return (low + STEP).reshape(width, 1, per * nblocks * groups)


def lane_gather(x, index):
    dims = lax.GatherDimensionNumbers(
        offset_dims=(),
        collapsed_slice_dims=(1,),
        start_index_map=(1,),
        operand_batching_dims=(0,),
        start_indices_batching_dims=(0,),
    )
    return lax.gather(
        x, index[..., None], dims, (1, 1), mode=lax.GatherScatterMode.PROMISE_IN_BOUNDS
    )


def kernel(
    width,
    jit_hbm,
    shift_hbm,
    sino_hbm,
    slab_hbm,
    base_hbm,
    out_ref,
    jit_ref,
    shift_ref,
    sino_ref,
    slab,
    base,
    chunks,
    msgs,
    tab,
    acc,
    fin,
    snd,
    rcv,
    lsem,
    wsem,
    sj,
    rj,
    s1,
    r1,
    s2,
    r2,
):
    me = lax.axis_index("blk")
    ang_dev, slices, bins = sino_ref.shape
    rows_dev = out_ref.shape[0]
    angles = width * ang_dev
    nrows = width * rows_dev
    nblocks = bins // LANES
    nspans = bins // BLOCK
    depth = width // PLANE
    groups = acc.shape[0]
    zper = SUBS // rows_dev
    z, q = me // PLANE, me % PLANE
    half = (bins - 1) / 2

    def remote(src, dst, send, recv, dev):
        return pltpu.make_async_remote_copy(
            src_ref=src,
            dst_ref=dst,
            send_sem=send,
            recv_sem=recv,
            device_id={"blk": dev},
            device_id_type=MESH,
        )

    loads = [
        pltpu.make_async_copy(src, dst, lsem.at[i])
        for i, (src, dst) in enumerate(
            [
                (jit_hbm, jit_ref),
                (sino_hbm, sino_ref),
                (shift_hbm, shift_ref),
                (base_hbm.at[me], base),
            ]
        )
    ]
    kblocks = bins // 2 // BLOCK
    ntiles = slab.shape[0]
    cuts = [0]
    for piece in range(PIECES):
        cuts.append(min(ntiles, 1 + 2 * -(-(2 * kblocks - 1) * (piece + 1) // PIECES)))
    weights = [
        pltpu.make_async_copy(
            slab_hbm.at[cuts[n] : cuts[n + 1]], slab.at[cuts[n] : cuts[n + 1]], wsem.at[n]
        )
        for n in range(PIECES)
    ]
    for load in loads[:2] + weights + loads[2:]:
        load.start()

    barrier = pltpu.get_barrier_semaphore()

    @pl.loop(1, width)
    def _(i):
        pl.semaphore_signal(
            barrier, inc=1, device_id={"blk": (me + i) % width}, device_id_type=MESH
        )

    def peer(d):
        qx, qy = q % 2, q // 2
        return z * PLANE + (qx + d % 2) % 2 + 2 * ((qy + d // 2) % 2)

    jrow = msgs.at[0, SUBS : 2 * SUBS]

    def jplane(d):
        return remote(msgs.at[0], msgs.at[d], sj.at[d - 1], rj.at[d - 1], peer(d))

    def jnext(p):
        return remote(
            jrow, msgs.at[PLANE, SUBS : 2 * SUBS], sj.at[PLANE - 1 + p], rj.at[PLANE - 1],
            (z + 1) % depth * PLANE + p,
        )

    def jprev(p):
        return remote(
            jrow, msgs.at[PLANE + 1, SUBS : 2 * SUBS], sj.at[PLANE - 1 + p], rj.at[PLANE],
            (z + depth - 1) % depth * PLANE + p,
        )

    def share(d):
        return remote(chunks.at[0], chunks.at[d], s1.at[d - 1], r1.at[d - 1], peer(d))

    def give(zt, part):
        return remote(
            snd.at[part, zt], rcv.at[part, z], s2.at[part, zt], r2.at[part, z], zt * PLANE + q
        )

    def take(zs, part):
        return remote(
            snd.at[part, zs], rcv.at[part, zs], s2.at[part, zs], r2.at[part, zs], zs * PLANE + q
        )

    lane = lax.broadcasted_iota(jnp.int32, (SUBS, LANES), 1)
    sub = lax.broadcasted_iota(jnp.int32, (SUBS, LANES), 0)
    lanef = lane.astype(jnp.float32)
    tab[tab.shape[0] - 1] = jnp.zeros((SUBS, LANES), jnp.int32)

    loads[0].wait()
    mine = (lane % angles) - me * ang_dev
    msg = jnp.zeros((SUBS, LANES), jnp.float32)
    for i in range(ang_dev):
        msg = jnp.where(mine == i, jit_ref[0:1, i : i + 1].astype(jnp.float32), msg)
    msgs[0, SUBS : 2 * SUBS] = msg

    loads[1].wait()
    flat = jnp.concatenate(
        [sino_ref[i].astype(jnp.float32) for i in range(ang_dev)], axis=0
    )
    tiles = [flat[:, b * LANES : (b + 1) * LANES] for b in range(nblocks)]
    top = jnp.abs(tiles[0])
    for tile in tiles[1:]:
        top = jnp.maximum(top, jnp.abs(tile))
    top = jnp.broadcast_to(jnp.max(top, axis=1, keepdims=True), (SUBS, LANES))
    msgs[0, :SUBS] = jnp.maximum(top, 1e-30) * (0.51 / 32700)

    pl.semaphore_wait(barrier, width - 1)

    for d in (3, 1, 2):
        jplane(d).start()

    @pl.when(q == PLANE - 1)
    def _():
        for p in range(PLANE):
            jnext(p).start()

    @pl.when(q == 0)
    def _():
        for p in range(PLANE):
            jprev(p).start()

    split = []
    for p in range(2):
        index = (2 * lane + p) % LANES
        picked = [lane_gather(tile, index) for tile in tiles]
        split.append(
            [
                jnp.where(lane < LANES // 2, picked[2 * t], picked[2 * t + 1])
                for t in range(nspans)
            ]
        )
    lhs = [
        jnp.concatenate(
            [jnp.concatenate([part[2 * k], part[2 * k + 1]], axis=1) for k in range(kblocks)],
            axis=0,
        ).astype(jnp.bfloat16)
        for part in split
    ]
    total = [
        [split[1 - p][t] * 0.25 for t in range(nspans)] for p in range(2)
    ]
    ready = 0
    for d in range(2 * kblocks - 1):
        while cuts[ready] < 2 * d + 3:
            weights[ready].wait()
            ready += 1
        for p in range(2):
            up = jnp.concatenate([slab[2 * d + 1, p], slab[2 * d + 2, p]], axis=1)
            down = jnp.concatenate([slab[2 * d, p], slab[2 * d + 1, p]], axis=1)
            prod = jnp.dot(
                lhs[p], jnp.concatenate([up, down], axis=0), preferred_element_type=jnp.float32
            )
            for i in range(kblocks):
                j = d - (kblocks - 1) + i
                if 0 <= j < kblocks:
                    for n in range(2):
                        total[p][2 * j + n] = (
                            total[p][2 * j + n]
                            + prod[i * SUBS : (i + 1) * SUBS, n * LANES : (n + 1) * LANES]
                        )
    for t in range(nspans):
        chunks[0, :, t * LANES : (t + 1) * LANES] = jnp.concatenate(
            [total[1][t], total[0][t]], axis=0
        ).astype(jnp.bfloat16)

    for d in (3, 1, 2):
        share(d).start()

    for d in range(1, PLANE):
        jplane(d).wait_recv()
    jnext(0).wait_recv()
    jprev(0).wait_recv()
    loads[2].wait()
    loads[3].wait()

    jit = msgs[0, SUBS : 2 * SUBS]
    for i in range(1, PLANE + 2):
        jit = jit + msgs[i, SUBS : 2 * SUBS]
    ahead = pltpu.roll(jit, LANES - 1, 1)
    behind = pltpu.roll(jit, 1, 1)
    weight = (1.0 + (ahead - behind) * 1.5) * (4.0 / math.sqrt(angles) / 65536)
    theta = ((lane % angles).astype(jnp.float32) + jit) * math.pi / angles
    cosine = jnp.cos(theta) * 0.5
    sine = jnp.sin(theta) * 0.5
    lead = sub % slices < slices // 2
    ypos = []
    for g in range(groups):
        row = ((sub % zper + g * zper) * PLANE + q) * rows_dev + sub // zper
        ypos.append(row.astype(jnp.float32) - (nrows - 1) / 2)

    def spread(d):
        inverse = 1.0 / msgs[d, :SUBS]
        words = []
        for t in range(nspans):
            both = chunks[d, :, t * LANES : (t + 1) * LANES].astype(jnp.float32)
            even = jnp.round(both[:SUBS] * inverse).astype(jnp.int32)
            odd = jnp.round(both[SUBS:] * inverse).astype(jnp.int32)
            high = jnp.where(lead, even, pltpu.roll(odd, 2, 0))
            low = jnp.where(lead, pltpu.roll(even, SUBS - 2, 0), odd)
            words.append(lax.shift_left(high, 16) + low)
            tab[4 * t + 1] = words[-1]
        for j in range(1, 4):
            cut = LANES - 32 * j
            turned = [pltpu.roll(word, cut, 1) for word in words]
            for t in range(nspans):
                after = turned[t + 1] if t + 1 < nspans else 0
                tab[4 * t + j + 1] = jnp.where(lane < cut, turned[t], after)
            if j == 3:
                tab[0] = jnp.where(lane < cut, 0, turned[0])

    def angle(d, i):
        first = peer(d) * ang_dev + i
        pick = jnp.full((SUBS, LANES), first, jnp.int32)
        cosb, sinb, wt = (lane_gather(x, pick) for x in (cosine, sine, weight))
        parts = [lanef * cosb + ypos[g] * sinb for g in range(groups)]
        scales = []
        for s in range(slices):
            line = jnp.broadcast_to(
                msgs[d, i * slices + s : i * slices + s + 1], (SUBS, LANES)
            )
            scales.append(line * wt)
        return cosb, parts, scales

    def line(slot, row):
        return jnp.broadcast_to(tab[slot, row : row + 1], (SUBS, LANES))

    def project(d, known, g, b):
        pc = peer(d)
        qc = pc - z * PLANE
        sums = [None] * slices
        for i in range(ang_dev):
            cosb, parts, scales = known[i]
            moved = shift_ref[pc * ang_dev + i]
            slot = base[0, ((qc * ang_dev + i) * nblocks + b) * groups + g]
            slot = lax.shift_right_arithmetic(slot + moved, 6)
            offset = (moved - slot * STEP).astype(jnp.float32) * 0.5 + (half + STEP) * 0.5
            h = cosb * (b * LANES - half) + parts[g] + offset
            odd = h.astype(jnp.int32)
            even = (h + 0.5).astype(jnp.int32)
            frac = jnp.abs(h - even.astype(jnp.float32)) * 2.0
            pairs = slices // 2
            evens = [lane_gather(line(slot, i * slices + s), even) for s in range(pairs)]
            odds = [lane_gather(line(slot, i * slices + pairs + s), odd) for s in range(pairs)]
            for s in range(slices):
                e, o = evens[s % pairs], odds[s % pairs]
                if s >= pairs:
                    e, o = lax.shift_left(e, 16), lax.shift_left(o, 16)
                e, o = e.astype(jnp.float32), o.astype(jnp.float32)
                got = (e + frac * (o - e)) * scales[s]
                sums[s] = got if sums[s] is None else sums[s] + got
        return sums

    spread(0)
    known = [angle(0, i) for i in range(ang_dev)]
    for b in range(nblocks):
        for g in range(groups):
            for s, val in enumerate(project(0, known, g, b)):
                acc[g, s, b] = val

    @pl.loop(1, PLANE - 1)
    def _(d):
        share(d).wait_recv()
        spread(d)
        known = [angle(d, i) for i in range(ang_dev)]
        for b in range(nblocks):
            for g in range(groups):
                for s, val in enumerate(project(d, known, g, b)):
                    acc[g, s, b] += val

    d = PLANE - 1
    share(d).wait_recv()
    spread(d)
    known = [angle(d, i) for i in range(ang_dev)]
    pos = sub % zper
    ntile = nblocks // 2 // PARTS
    for part in range(PARTS):
        for t in range(ntile):
            for g in range(groups):
                out = [[], [], [], []]
                for b in (2 * (part * ntile + t), 2 * (part * ntile + t) + 1):
                    v = [acc[g, s, b] + x for s, x in enumerate(project(d, known, g, b))]
                    w = [None] * 4
                    for s in range(2):
                        w[s] = jnp.where(pos < 2, v[s], pltpu.roll(v[s + 2], 2, 0))
                        w[s + 2] = jnp.where(pos < 2, pltpu.roll(v[s], SUBS - 2, 0), v[s + 2])
                    for s in (0, 2):
                        lo = jnp.where(pos % 2 < 1, w[s], pltpu.roll(w[s + 1], 1, 0))
                        hi = jnp.where(pos % 2 < 1, pltpu.roll(w[s], SUBS - 1, 0), w[s + 1])
                        for n, val in ((s, lo), (s + 1, hi)):
                            fin[g * zper + n, b] = val
                            out[n].append(val)
                for n in range(4):
                    snd[part, g * zper + n, :, t * LANES : (t + 1) * LANES] = jnp.concatenate(
                        out[n], axis=0
                    ).astype(jnp.bfloat16)

        @pl.loop(0, depth)
        def _(zt):
            @pl.when(zt != z)
            def _():
                give(zt, part).start()

    for part in range(PARTS):
        @pl.loop(1, depth)
        def _(k):
            take((z + k) % depth, part).wait_recv()

        for t in range(ntile):
            b = 2 * (part * ntile + t)
            sums = [fin[z, b], fin[z, b + 1]]
            for k in range(1, depth):
                both = rcv[part, (z + k) % depth, :, t * LANES : (t + 1) * LANES]
                both = both.astype(jnp.float32)
                sums = [sums[0] + both[:SUBS], sums[1] + both[SUBS:]]
            for j in range(2):
                cols = slice((b + j) * LANES, (b + j + 1) * LANES)
                for r in range(rows_dev):
                    out_ref[r, :, cols] = sums[j][r * slices : (r + 1) * slices]

    for d in range(1, PLANE):
        jplane(d).wait_send()
        share(d).wait_send()

    @pl.when(q == PLANE - 1)
    def _():
        for p in range(PLANE):
            jnext(p).wait_send()

    @pl.when(q == 0)
    def _():
        for p in range(PLANE):
            jprev(p).wait_send()

    for part in range(PARTS):
        @pl.loop(1, depth)
        def _(k):
            give((z + k) % depth, part).wait_send()


def body(sinogram, jitter, shift):
    width = lax.axis_size("blk")
    ang_dev, slices, bins = sinogram.shape
    angles = shift.shape[0]
    rows_dev = SUBS // slices
    depth = width // PLANE
    assert ang_dev == 2 and rows_dev == 2 and slices == 4 and LANES % angles == 0
    assert width % (PLANE * 4) == 0 and bins % (2 * BLOCK) == 0
    groups = depth * rows_dev // SUBS
    nblocks = bins // LANES
    anywhere = pl.BlockSpec(memory_space=pl.ANY)
    dma = pltpu.SemaphoreType.DMA
    slab = jnp.asarray(ramp_slab(bins))
    base = jnp.asarray(window_base(width, ang_dev, rows_dev, bins))
    return pl.pallas_call(
        functools.partial(kernel, width),
        out_shape=pltpu.VMEM((rows_dev, slices, bins), jnp.float32),
        in_specs=[anywhere] * 5,
        out_specs=pl.BlockSpec(memory_space=pltpu.VMEM),
        scratch_shapes=[
            pltpu.VMEM((1, ang_dev), jnp.bfloat16),
            pltpu.SMEM((angles,), jnp.int32),
            pltpu.VMEM((ang_dev, slices, bins), jnp.bfloat16),
            pltpu.VMEM(slab.shape, jnp.bfloat16),
            pltpu.SMEM(base.shape[1:], jnp.int32),
            pltpu.VMEM((PLANE, 2 * SUBS, bins // 2), jnp.bfloat16),
            pltpu.VMEM((PLANE + 2, 2 * SUBS, LANES), jnp.float32),
            pltpu.VMEM((bins // STEP + 2, SUBS, LANES), jnp.int32),
            pltpu.VMEM((groups, slices, nblocks, SUBS, LANES), jnp.float32),
            pltpu.VMEM((depth, nblocks, SUBS, LANES), jnp.float32),
            pltpu.VMEM((PARTS, depth, 2 * SUBS, bins // 2 // PARTS), jnp.bfloat16),
            pltpu.VMEM((PARTS, depth, 2 * SUBS, bins // 2 // PARTS), jnp.bfloat16),
            dma((4,)),
            dma((PIECES,)),
            dma((2 * PLANE - 1,)),
            dma((PLANE + 1,)),
            dma((PLANE - 1,)),
            dma((PLANE - 1,)),
            dma((PARTS, depth)),
            dma((PARTS, depth)),
        ],
        compiler_params=pltpu.CompilerParams(collective_id=0, has_side_effects=True),
    )(jitter.reshape(1, ang_dev), shift, sinogram, slab, base)


def solution(mesh):
    in_specs = (P("blk", "slab", None), P("blk"), P())
    out_specs = P("blk", "slab", None)
    return jax.shard_map(body, mesh=mesh, in_specs=in_specs, out_specs=out_specs, check_vma=False)
```

time: 18.5 us -> 17.8 us (0.962)
  Pallas kernels: 17.7 us -> 17 us
    pallas_call x1, Pallas kernels: 17.7 us -> 17 us  [body(): pl.pallas_call(functools.partial(kernel, width), out_shape=pltpu.VMEM((ro...]
where the time goes in v2:
time: 17.8 us; the launch traced here: 17.7 us
  Pallas kernels  17 us (96%)
  local copies, waits for them, and re-layouts  0.63 us (4%)
    pallas_call x1, Pallas kernels, body(): pl.pallas_call(functools.partial(kernel, width), out_shape=pltpu.VMEM((ro...  17 us
    unnamed x1, local copies, waits for them, and re-layouts  0.63 us

profile of v2, /device:TPU:0, one launch (start us, length us, event | category | flops | bytes accessed | tf_op | source)
XLA Modules:
  0.0 17.7 jit_solution(1923960680645205061)
XLA Ops:
  0.0 17.0 %shard_map.55 = f32[2,4,2048]{2,1,0:T(4,128)S(1)} custom-call(bf16[1,2]{1,0:T(2,128)(2,1)} %bitcast.1, s32[32]{0:T(128)} %shift_hbm.1, bf16[2,4,2048]{2,1,0:T(4,128)(2,1)} %sino_hbm.1, bf16[15,2,128,128]{3,2,1,0:T(8,128)(2,1)} %constant.4.clone.slab_hbm, s32[16,1,128]{2,1,0:T(1,128)} %constant.5.clone.base_hbm), custom_call_target="tpu_custom_call" | custom-call | tf_op jit(solution)/shard_map/pallas_call | solution.py:463
  17.0 0.6 %copy.7 = f32[2,4,2048]{2,1,0:T(4,128)} copy(f32[2,4,2048]{2,1,0:T(4,128)S(1)} %shard_map.55) | data formatting | bytes 131072

commit v3 on v2

--- a/solution.py
+++ b/solution.py
@@ -88,6 +88,8 @@
     msgs,
     tab,
     acc,
+    own,
+    wvec,
     fin,
     snd,
     rcv,
@@ -150,15 +152,35 @@
 
     barrier = pltpu.get_barrier_semaphore()
 
-    @pl.loop(1, width)
-    def _(i):
-        pl.semaphore_signal(
-            barrier, inc=1, device_id={"blk": (me + i) % width}, device_id_type=MESH
-        )
+    qx, qy = q % 2, q // 2
+    ends = PLANE - 1
 
     def peer(d):
-        qx, qy = q % 2, q // 2
         return z * PLANE + (qx + d % 2) % 2 + 2 * ((qy + d // 2) % 2)
+
+    def hello(dev):
+        pl.semaphore_signal(barrier, inc=1, device_id={"blk": dev}, device_id_type=MESH)
+
+    for d in (3, 1, 2):
+        hello(peer(d))
+
+    @pl.loop(1, depth)
+    def _(k):
+        hello((z + k) % depth * PLANE + q)
+
+    @pl.when(q != ends)
+    def _():
+        hello((z + depth - 1) % depth * PLANE + ends)
+
+    @pl.when((q != 0) & (z < depth - 1))
+    def _():
+        hello((z + 1) * PLANE)
+
+    greeted = (
+        ends + depth - 1
+        + ends * (q // ends)
+        + ends * ((PLANE - 1 - q) // ends) * ((z + depth - 1) // depth)
+    )
 
     jrow = msgs.at[0, SUBS : 2 * SUBS]
 
@@ -174,7 +196,13 @@
     def jprev(p):
         return remote(
             jrow, msgs.at[PLANE + 1, SUBS : 2 * SUBS], sj.at[PLANE - 1 + p], rj.at[PLANE],
-            (z + depth - 1) % depth * PLANE + p,
+            (z - 1) * PLANE + p,
+        )
+
+    def jwrap():
+        return remote(
+            msgs.at[q, SUBS : 2 * SUBS], msgs.at[PLANE + 1, SUBS : 2 * SUBS],
+            sj.at[2 * PLANE - 1], rj.at[PLANE], (depth - 1) * PLANE + q,
         )
 
     def share(d):
@@ -194,6 +222,10 @@
     sub = lax.broadcasted_iota(jnp.int32, (SUBS, LANES), 0)
     lanef = lane.astype(jnp.float32)
     tab[tab.shape[0] - 1] = jnp.zeros((SUBS, LANES), jnp.int32)
+    for g in range(groups):
+        for s in range(slices):
+            for b in range(nblocks):
+                acc[g, s, b] = jnp.zeros((SUBS, LANES), jnp.float32)
 
     loads[0].wait()
     mine = (lane % angles) - me * ang_dev
@@ -213,7 +245,7 @@
     top = jnp.broadcast_to(jnp.max(top, axis=1, keepdims=True), (SUBS, LANES))
     msgs[0, :SUBS] = jnp.maximum(top, 1e-30) * (0.51 / 32700)
 
-    pl.semaphore_wait(barrier, width - 1)
+    pl.semaphore_wait(barrier, greeted)
 
     for d in (3, 1, 2):
         jplane(d).start()
@@ -223,10 +255,14 @@
         for p in range(PLANE):
             jnext(p).start()
 
-    @pl.when(q == 0)
+    @pl.when((q == 0) & (z > 0))
     def _():
         for p in range(PLANE):
             jprev(p).start()
+
+    @pl.when((q == 0) & (z == 0))
+    def _():
+        jwrap().start()
 
     split = []
     for p in range(2):
@@ -275,22 +311,18 @@
     for d in (3, 1, 2):
         share(d).start()
 
-    for d in range(1, PLANE):
-        jplane(d).wait_recv()
-    jnext(0).wait_recv()
-    jprev(0).wait_recv()
     loads[2].wait()
     loads[3].wait()
 
-    jit = msgs[0, SUBS : 2 * SUBS]
-    for i in range(1, PLANE + 2):
-        jit = jit + msgs[i, SUBS : 2 * SUBS]
-    ahead = pltpu.roll(jit, LANES - 1, 1)
-    behind = pltpu.roll(jit, 1, 1)
-    weight = (1.0 + (ahead - behind) * 1.5) * (4.0 / math.sqrt(angles) / 65536)
-    theta = ((lane % angles).astype(jnp.float32) + jit) * math.pi / angles
-    cosine = jnp.cos(theta) * 0.5
-    sine = jnp.sin(theta) * 0.5
+    def waves(jit):
+        theta = ((lane % angles).astype(jnp.float32) + jit) * math.pi / angles
+        return jnp.cos(theta) * 0.5, jnp.sin(theta) * 0.5
+
+    def weigh(jit):
+        ahead = pltpu.roll(jit, LANES - 1, 1)
+        behind = pltpu.roll(jit, 1, 1)
+        return (1.0 + (ahead - behind) * 1.5) * (4.0 / math.sqrt(angles))
+
     lead = sub % slices < slices // 2
     ypos = []
     for g in range(groups):
@@ -317,17 +349,16 @@
             if j == 3:
                 tab[0] = jnp.where(lane < cut, 0, turned[0])
 
-    def angle(d, i):
-        first = peer(d) * ang_dev + i
-        pick = jnp.full((SUBS, LANES), first, jnp.int32)
-        cosb, sinb, wt = (lane_gather(x, pick) for x in (cosine, sine, weight))
+    def angle(d, i, wave, weight):
+        pick = jnp.full((SUBS, LANES), peer(d) * ang_dev + i, jnp.int32)
+        cosb, sinb = (lane_gather(x, pick) for x in wave)
         parts = [lanef * cosb + ypos[g] * sinb for g in range(groups)]
+        wt = 1.0 if weight is None else lane_gather(weight, pick)
         scales = []
         for s in range(slices):
-            line = jnp.broadcast_to(
-                msgs[d, i * slices + s : i * slices + s + 1], (SUBS, LANES)
-            )
-            scales.append(line * wt)
+            row = i * slices + s
+            scale = jnp.broadcast_to(msgs[d, row : row + 1], (SUBS, LANES))
+            scales.append(scale * (wt * (1.0 / 65536)))
         return cosb, parts, scales
 
     def line(slot, row):
@@ -336,7 +367,7 @@
     def project(d, known, g, b):
         pc = peer(d)
         qc = pc - z * PLANE
-        sums = [None] * slices
+        sums = []
         for i in range(ang_dev):
             cosb, parts, scales = known[i]
             moved = shift_ref[pc * ang_dev + i]
@@ -350,36 +381,72 @@
             pairs = slices // 2
             evens = [lane_gather(line(slot, i * slices + s), even) for s in range(pairs)]
             odds = [lane_gather(line(slot, i * slices + pairs + s), odd) for s in range(pairs)]
+            got = []
             for s in range(slices):
                 e, o = evens[s % pairs], odds[s % pairs]
                 if s >= pairs:
                     e, o = lax.shift_left(e, 16), lax.shift_left(o, 16)
                 e, o = e.astype(jnp.float32), o.astype(jnp.float32)
-                got = (e + frac * (o - e)) * scales[s]
-                sums[s] = got if sums[s] is None else sums[s] + got
+                got.append((e + frac * (o - e)) * scales[s])
+            sums.append(got)
         return sums
 
     spread(0)
-    known = [angle(0, i) for i in range(ang_dev)]
+    wave = waves(msgs[0, SUBS : 2 * SUBS])
+    known = [angle(0, i, wave, None) for i in range(ang_dev)]
     for b in range(nblocks):
         for g in range(groups):
-            for s, val in enumerate(project(0, known, g, b)):
-                acc[g, s, b] = val
-
-    @pl.loop(1, PLANE - 1)
-    def _(d):
+            for i, got in enumerate(project(0, known, g, b)):
+                for s in range(slices):
+                    own[i, g, s, b] = got[s]
+
+    for d in range(1, PLANE):
+        jplane(d).wait_recv()
+
+    @pl.when((q > 0) & (z == 0))
+    def _():
+        jwrap().start()
+
+    def known_jitter(slots):
+        jit = msgs[0, SUBS : 2 * SUBS]
+        for i in range(1, slots):
+            jit = jit + msgs[i, SUBS : 2 * SUBS]
+        return jit
+
+    for i, x in enumerate(waves(known_jitter(PLANE))):
+        wvec[i] = x
+    wvec[2] = weigh(known_jitter(PLANE))
+
+    order = [1 + 2 * ((qx + qy) % 2), 2 - qx * (1 - qy)]
+    order.append(6 - order[0] - order[1])
+
+    @pl.loop(0, PLANE - 2)
+    def _(step):
+        @pl.when(step == 1)
+        def _():
+            jnext(0).wait_recv()
+            wvec[2] = weigh(known_jitter(PLANE + 1))
+
+        d = order[0] + step * (order[1] - order[0])
         share(d).wait_recv()
         spread(d)
-        known = [angle(d, i) for i in range(ang_dev)]
+        known = [angle(d, i, (wvec[0], wvec[1]), wvec[2]) for i in range(ang_dev)]
         for b in range(nblocks):
             for g in range(groups):
-                for s, val in enumerate(project(d, known, g, b)):
-                    acc[g, s, b] += val
-
-    d = PLANE - 1
+                first, second = project(d, known, g, b)
+                for s in range(slices):
+                    acc[g, s, b] += first[s] + second[s]
+
+    d = order[2]
+    jprev(0).wait_recv()
     share(d).wait_recv()
+    weight = weigh(known_jitter(PLANE + 2))
     spread(d)
-    known = [angle(d, i) for i in range(ang_dev)]
+    known = [angle(d, i, (wvec[0], wvec[1]), weight) for i in range(ang_dev)]
+    mine = [
+        lane_gather(weight, jnp.full((SUBS, LANES), me * ang_dev + i, jnp.int32))
+        for i in range(ang_dev)
+    ]
     pos = sub % zper
     ntile = nblocks // 2 // PARTS
     for part in range(PARTS):
@@ -387,7 +454,12 @@
             for g in range(groups):
                 out = [[], [], [], []]
                 for b in (2 * (part * ntile + t), 2 * (part * ntile + t) + 1):
-                    v = [acc[g, s, b] + x for s, x in enumerate(project(d, known, g, b))]
+                    first, second = project(d, known, g, b)
+                    v = [
+                        (acc[g, s, b] + mine[0] * own[0, g, s, b])
+                        + (mine[1] * own[1, g, s, b] + (first[s] + second[s]))
+                        for s in range(slices)
+                    ]
                     w = [None] * 4
                     for s in range(2):
                         w[s] = jnp.where(pos < 2, v[s], pltpu.roll(v[s + 2], 2, 0))
@@ -435,10 +507,14 @@
         for p in range(PLANE):
             jnext(p).wait_send()
 
-    @pl.when(q == 0)
+    @pl.when((q == 0) & (z > 0))
     def _():
         for p in range(PLANE):
             jprev(p).wait_send()
+
+    @pl.when(z == 0)
+    def _():
+        jwrap().wait_send()
 
     for part in range(PARTS):
         @pl.loop(1, depth)
@@ -475,12 +551,14 @@
             pltpu.VMEM((PLANE + 2, 2 * SUBS, LANES), jnp.float32),
             pltpu.VMEM((bins // STEP + 2, SUBS, LANES), jnp.int32),
             pltpu.VMEM((groups, slices, nblocks, SUBS, LANES), jnp.float32),
+            pltpu.VMEM((ang_dev, groups, slices, nblocks, SUBS, LANES), jnp.float32),
+            pltpu.VMEM((3, SUBS, LANES), jnp.float32),
             pltpu.VMEM((depth, nblocks, SUBS, LANES), jnp.float32),
             pltpu.VMEM((PARTS, depth, 2 * SUBS, bins // 2 // PARTS), jnp.bfloat16),
             pltpu.VMEM((PARTS, depth, 2 * SUBS, bins // 2 // PARTS), jnp.bfloat16),
             dma((4,)),
             dma((PIECES,)),
-            dma((2 * PLANE - 1,)),
+            dma((2 * PLANE,)),
             dma((PLANE + 1,)),
             dma((PLANE - 1,)),
             dma((PLANE - 1,)),

time: 17.8 us -> 16.4 us (0.921)
  the two profiles are of different devices: /device:TPU:0 before, /device:TPU:4 now
where the time goes in v3:
time: 16.4 us; the launch traced here: 16.2 us
  Pallas kernels  15.6 us (95%)
  local copies, waits for them, and re-layouts  0.63 us (4%)
    pallas_call x1, Pallas kernels, body(): pl.pallas_call(functools.partial(kernel, width), out_shape=pltpu.VMEM((ro...  15.6 us
    unnamed x1, local copies, waits for them, and re-layouts  0.63 us

profile of v3, /device:TPU:4, one launch (start us, length us, event | category | flops | bytes accessed | tf_op | source)
XLA Modules:
  0.0 16.2 jit_solution(9896763332388766732)
XLA Ops:
  0.0 15.6 %shard_map.55 = f32[2,4,2048]{2,1,0:T(4,128)S(1)} custom-call(bf16[1,2]{1,0:T(2,128)(2,1)} %bitcast.1, s32[32]{0:T(128)} %shift_hbm.1, bf16[2,4,2048]{2,1,0:T(4,128)(2,1)} %sino_hbm.1, bf16[15,2,128,128]{3,2,1,0:T(8,128)(2,1)} %constant.4.clone.slab_hbm, s32[16,1,128]{2,1,0:T(1,128)} %constant.5.clone.base_hbm), custom_call_target="tpu_custom_call" | custom-call | tf_op jit(solution)/shard_map/pallas_call | solution.py:539
  15.6 0.6 %copy.7 = f32[2,4,2048]{2,1,0:T(4,128)} copy(f32[2,4,2048]{2,1,0:T(4,128)S(1)} %shard_map.55) | data formatting | bytes 131072

commit v4 on v3

--- a/solution.py
+++ b/solution.py
@@ -16,8 +16,9 @@
 STEP = 64
 JITTER = 0.29882812
 SHIFT = 8
-PIECES = 4
-PARTS = 2
+PIECES = 2
+PARTS = 1
+SENDS = (3, 1, 2)
 MESH = pl.DeviceIdType.MESH
 
 
@@ -87,9 +88,7 @@
     chunks,
     msgs,
     tab,
-    acc,
-    own,
-    wvec,
+    held,
     fin,
     snd,
     rcv,
@@ -110,7 +109,7 @@
     nblocks = bins // LANES
     nspans = bins // BLOCK
     depth = width // PLANE
-    groups = acc.shape[0]
+    groups = held.shape[2]
     zper = SUBS // rows_dev
     z, q = me // PLANE, me % PLANE
     half = (bins - 1) / 2
@@ -222,17 +221,20 @@
     sub = lax.broadcasted_iota(jnp.int32, (SUBS, LANES), 0)
     lanef = lane.astype(jnp.float32)
     tab[tab.shape[0] - 1] = jnp.zeros((SUBS, LANES), jnp.int32)
-    for g in range(groups):
-        for s in range(slices):
-            for b in range(nblocks):
-                acc[g, s, b] = jnp.zeros((SUBS, LANES), jnp.float32)
 
     loads[0].wait()
     mine = (lane % angles) - me * ang_dev
     msg = jnp.zeros((SUBS, LANES), jnp.float32)
     for i in range(ang_dev):
         msg = jnp.where(mine == i, jit_ref[0:1, i : i + 1].astype(jnp.float32), msg)
-    msgs[0, SUBS : 2 * SUBS] = msg
+    theta = ((lane % angles).astype(jnp.float32) + msg) * math.pi / angles
+    waves = [jnp.cos(theta) * 0.5, jnp.sin(theta) * 0.5]
+    body = msg
+    for i in range(ang_dev):
+        pick = jnp.full((SUBS, LANES), me * ang_dev + i, jnp.int32)
+        for n in range(2):
+            body = jnp.where(sub == 1 + 2 * i + n, lane_gather(waves[n], pick), body)
+    msgs[0, SUBS : 2 * SUBS] = body
 
     loads[1].wait()
     flat = jnp.concatenate(
@@ -244,25 +246,6 @@
         top = jnp.maximum(top, jnp.abs(tile))
     top = jnp.broadcast_to(jnp.max(top, axis=1, keepdims=True), (SUBS, LANES))
     msgs[0, :SUBS] = jnp.maximum(top, 1e-30) * (0.51 / 32700)
-
-    pl.semaphore_wait(barrier, greeted)
-
-    for d in (3, 1, 2):
-        jplane(d).start()
-
-    @pl.when(q == PLANE - 1)
-    def _():
-        for p in range(PLANE):
-            jnext(p).start()
-
-    @pl.when((q == 0) & (z > 0))
-    def _():
-        for p in range(PLANE):
-            jprev(p).start()
-
-    @pl.when((q == 0) & (z == 0))
-    def _():
-        jwrap().start()
 
     split = []
     for p in range(2):
@@ -308,20 +291,30 @@
             [total[1][t], total[0][t]], axis=0
         ).astype(jnp.bfloat16)
 
+    pl.semaphore_wait(barrier, greeted)
+
     for d in (3, 1, 2):
+        jplane(d).start()
+
+    @pl.when(q == PLANE - 1)
+    def _():
+        for p in range(PLANE):
+            jnext(p).start()
+
+    @pl.when((q == 0) & (z > 0))
+    def _():
+        for p in range(PLANE):
+            jprev(p).start()
+
+    @pl.when((q == 0) & (z == 0))
+    def _():
+        jwrap().start()
+
+    for d in SENDS:
         share(d).start()
 
     loads[2].wait()
     loads[3].wait()
-
-    def waves(jit):
-        theta = ((lane % angles).astype(jnp.float32) + jit) * math.pi / angles
-        return jnp.cos(theta) * 0.5, jnp.sin(theta) * 0.5
-
-    def weigh(jit):
-        ahead = pltpu.roll(jit, LANES - 1, 1)
-        behind = pltpu.roll(jit, 1, 1)
-        return (1.0 + (ahead - behind) * 1.5) * (4.0 / math.sqrt(angles))
 
     lead = sub % slices < slices // 2
     ypos = []
@@ -349,16 +342,13 @@
             if j == 3:
                 tab[0] = jnp.where(lane < cut, 0, turned[0])
 
-    def angle(d, i, wave, weight):
-        pick = jnp.full((SUBS, LANES), peer(d) * ang_dev + i, jnp.int32)
-        cosb, sinb = (lane_gather(x, pick) for x in wave)
+    def spoken(d, row):
+        return jnp.broadcast_to(msgs[d, row : row + 1], (SUBS, LANES))
+
+    def angle(d, i):
+        cosb, sinb = (spoken(d, SUBS + 1 + 2 * i + n) for n in range(2))
         parts = [lanef * cosb + ypos[g] * sinb for g in range(groups)]
-        wt = 1.0 if weight is None else lane_gather(weight, pick)
-        scales = []
-        for s in range(slices):
-            row = i * slices + s
-            scale = jnp.broadcast_to(msgs[d, row : row + 1], (SUBS, LANES))
-            scales.append(scale * (wt * (1.0 / 65536)))
+        scales = [spoken(d, i * slices + s) * (1.0 / 65536) for s in range(slices)]
         return cosb, parts, scales
 
     def line(slot, row):
@@ -391,62 +381,53 @@
             sums.append(got)
         return sums
 
-    spread(0)
-    wave = waves(msgs[0, SUBS : 2 * SUBS])
-    known = [angle(0, i, wave, None) for i in range(ang_dev)]
-    for b in range(nblocks):
-        for g in range(groups):
-            for i, got in enumerate(project(0, known, g, b)):
-                for s in range(slices):
-                    own[i, g, s, b] = got[s]
-
-    for d in range(1, PLANE):
-        jplane(d).wait_recv()
-
-    @pl.when((q > 0) & (z == 0))
-    def _():
-        jwrap().start()
-
-    def known_jitter(slots):
-        jit = msgs[0, SUBS : 2 * SUBS]
-        for i in range(1, slots):
-            jit = jit + msgs[i, SUBS : 2 * SUBS]
-        return jit
-
-    for i, x in enumerate(waves(known_jitter(PLANE))):
-        wvec[i] = x
-    wvec[2] = weigh(known_jitter(PLANE))
-
-    order = [1 + 2 * ((qx + qy) % 2), 2 - qx * (1 - qy)]
-    order.append(6 - order[0] - order[1])
-
-    @pl.loop(0, PLANE - 2)
-    def _(step):
-        @pl.when(step == 1)
-        def _():
-            jnext(0).wait_recv()
-            wvec[2] = weigh(known_jitter(PLANE + 1))
-
-        d = order[0] + step * (order[1] - order[0])
-        share(d).wait_recv()
+    def keep(d):
         spread(d)
-        known = [angle(d, i, (wvec[0], wvec[1]), wvec[2]) for i in range(ang_dev)]
+        known = [angle(d, i) for i in range(ang_dev)]
         for b in range(nblocks):
             for g in range(groups):
-                first, second = project(d, known, g, b)
-                for s in range(slices):
-                    acc[g, s, b] += first[s] + second[s]
-
-    d = order[2]
+                for i, got in enumerate(project(d, known, g, b)):
+                    for s in range(slices):
+                        held[d, i, g, s, b] = got[s]
+
+    keep(0)
+
+    @pl.when((q > 0) & (z == 0))
+    def _():
+        jplane(q).wait_recv()
+        jwrap().start()
+
+    @pl.loop(1, PLANE - 1)
+    def _(d):
+        @pl.when((z > 0) | (q != d))
+        def _():
+            jplane(d).wait_recv()
+
+        share(d).wait_recv()
+        keep(d)
+
+    d = PLANE - 1
+
+    @pl.when((z > 0) | (q != d))
+    def _():
+        jplane(d).wait_recv()
+
+    jnext(0).wait_recv()
     jprev(0).wait_recv()
     share(d).wait_recv()
-    weight = weigh(known_jitter(PLANE + 2))
+    jit = sum(spoken(i, SUBS) for i in range(PLANE + 2))
+    ahead = pltpu.roll(jit, LANES - 1, 1)
+    behind = pltpu.roll(jit, 1, 1)
+    weight = (1.0 + (ahead - behind) * 1.5) * (4.0 / math.sqrt(angles))
+    weight = [
+        [
+            lane_gather(weight, jnp.full((SUBS, LANES), peer(n) * ang_dev + i, jnp.int32))
+            for i in range(ang_dev)
+        ]
+        for n in range(PLANE)
+    ]
     spread(d)
-    known = [angle(d, i, (wvec[0], wvec[1]), weight) for i in range(ang_dev)]
-    mine = [
-        lane_gather(weight, jnp.full((SUBS, LANES), me * ang_dev + i, jnp.int32))
-        for i in range(ang_dev)
-    ]
+    known = [angle(d, i) for i in range(ang_dev)]
     pos = sub % zper
     ntile = nblocks // 2 // PARTS
     for part in range(PARTS):
@@ -454,12 +435,15 @@
             for g in range(groups):
                 out = [[], [], [], []]
                 for b in (2 * (part * ntile + t), 2 * (part * ntile + t) + 1):
-                    first, second = project(d, known, g, b)
-                    v = [
-                        (acc[g, s, b] + mine[0] * own[0, g, s, b])
-                        + (mine[1] * own[1, g, s, b] + (first[s] + second[s]))
-                        for s in range(slices)
-                    ]
+                    got = project(d, known, g, b)
+                    v = []
+                    for s in range(slices):
+                        terms = [weight[d][i] * got[i][s] for i in range(ang_dev)]
+                        for n in range(PLANE - 1):
+                            terms += [weight[n][i] * held[n, i, g, s, b] for i in range(ang_dev)]
+                        while len(terms) > 1:
+                            terms = [x + y for x, y in zip(terms[::2], terms[1::2])]
+                        v += terms
                     w = [None] * 4
                     for s in range(2):
                         w[s] = jnp.where(pos < 2, v[s], pltpu.roll(v[s + 2], 2, 0))
@@ -550,9 +534,7 @@
             pltpu.VMEM((PLANE, 2 * SUBS, bins // 2), jnp.bfloat16),
             pltpu.VMEM((PLANE + 2, 2 * SUBS, LANES), jnp.float32),
             pltpu.VMEM((bins // STEP + 2, SUBS, LANES), jnp.int32),
-            pltpu.VMEM((groups, slices, nblocks, SUBS, LANES), jnp.float32),
-            pltpu.VMEM((ang_dev, groups, slices, nblocks, SUBS, LANES), jnp.float32),
-            pltpu.VMEM((3, SUBS, LANES), jnp.float32),
+            pltpu.VMEM((PLANE - 1, ang_dev, groups, slices, nblocks, SUBS, LANES), jnp.float32),
             pltpu.VMEM((depth, nblocks, SUBS, LANES), jnp.float32),
             pltpu.VMEM((PARTS, depth, 2 * SUBS, bins // 2 // PARTS), jnp.bfloat16),
             pltpu.VMEM((PARTS, depth, 2 * SUBS, bins // 2 // PARTS), jnp.bfloat16),

time: 16.4 us -> 15.2 us (0.927)
  the two profiles are of different devices: /device:TPU:4 before, /device:TPU:0 now
where the time goes in v4:
time: 15.2 us; the launch traced here: 15.1 us
  Pallas kernels  14.4 us (95%)
  local copies, waits for them, and re-layouts  0.63 us (4%)
    pallas_call x1, Pallas kernels, body(): pl.pallas_call(functools.partial(kernel, width), out_shape=pltpu.VMEM((ro...  14.4 us
    unnamed x1, local copies, waits for them, and re-layouts  0.63 us

profile of v4, /device:TPU:0, one launch (start us, length us, event | category | flops | bytes accessed | tf_op | source)
XLA Modules:
  0.0 15.1 jit_solution(5833233902210281048)
XLA Ops:
  0.0 14.4 %shard_map.55 = f32[2,4,2048]{2,1,0:T(4,128)S(1)} custom-call(bf16[1,2]{1,0:T(2,128)(2,1)} %bitcast.1, s32[32]{0:T(128)} %shift_hbm.1, bf16[2,4,2048]{2,1,0:T(4,128)(2,1)} %sino_hbm.1, bf16[15,2,128,128]{3,2,1,0:T(8,128)(2,1)} %constant.4.clone.slab_hbm, s32[16,1,128]{2,1,0:T(1,128)} %constant.5.clone.base_hbm), custom_call_target="tpu_custom_call" | custom-call | tf_op jit(solution)/shard_map/pallas_call | solution.py:523
  14.4 0.6 %copy.7 = f32[2,4,2048]{2,1,0:T(4,128)} copy(f32[2,4,2048]{2,1,0:T(4,128)S(1)} %shard_map.55) | data formatting | bytes 131072

commit v5 on v4

--- a/solution.py
+++ b/solution.py
@@ -16,21 +16,18 @@
 STEP = 64
 JITTER = 0.29882812
 SHIFT = 8
-PIECES = 2
+PIECES = 1
 PARTS = 1
-SENDS = (3, 1, 2)
+SENDS = (1, 2, 3)
 MESH = pl.DeviceIdType.MESH
 
 
 def ramp_slab(bins):
     span = bins // 2
-    first = -(span - LANES)
-    offset = np.arange(first, span, dtype=np.int32)[None, :] - np.arange(LANES, dtype=np.int32)[:, None]
-    both = 2 * np.stack([offset, offset - 1]) + 1
-    safe = both.astype(np.float32)
+    offset = np.arange(-span, span, dtype=np.int32)[None, :] - np.arange(LANES, dtype=np.int32)[:, None]
+    safe = (2 * offset + 1).astype(np.float32)
     slab = (np.float32(-1.0) / (np.float32(math.pi**2) * safe * safe)).astype(jnp.bfloat16)
-    tiles = slab.reshape(2, LANES, -1, LANES)
-    return np.ascontiguousarray(tiles.transpose(2, 0, 1, 3))
+    return np.ascontiguousarray(slab.reshape(LANES, -1, LANES).transpose(1, 0, 2))
 
 
 def window_base(width, ang_dev, rows_dev, bins):
@@ -139,7 +136,7 @@
     ntiles = slab.shape[0]
     cuts = [0]
     for piece in range(PIECES):
-        cuts.append(min(ntiles, 1 + 2 * -(-(2 * kblocks - 1) * (piece + 1) // PIECES)))
+        cuts.append(2 + 2 * -(-(2 * kblocks - 1) * (piece + 1) // PIECES))
     weights = [
         pltpu.make_async_copy(
             slab_hbm.at[cuts[n] : cuts[n + 1]], slab.at[cuts[n] : cuts[n + 1]], wsem.at[n]
@@ -223,69 +220,75 @@
     tab[tab.shape[0] - 1] = jnp.zeros((SUBS, LANES), jnp.int32)
 
     loads[0].wait()
+    loads[1].wait()
+    flat = jnp.concatenate(
+        [sino_ref[i].astype(jnp.float32) for i in range(ang_dev)], axis=0
+    )
+    tiles = [flat[:, b * LANES : (b + 1) * LANES] for b in range(nblocks)]
     mine = (lane % angles) - me * ang_dev
     msg = jnp.zeros((SUBS, LANES), jnp.float32)
     for i in range(ang_dev):
         msg = jnp.where(mine == i, jit_ref[0:1, i : i + 1].astype(jnp.float32), msg)
     theta = ((lane % angles).astype(jnp.float32) + msg) * math.pi / angles
     waves = [jnp.cos(theta) * 0.5, jnp.sin(theta) * 0.5]
-    body = msg
+    rows = msg
     for i in range(ang_dev):
         pick = jnp.full((SUBS, LANES), me * ang_dev + i, jnp.int32)
         for n in range(2):
-            body = jnp.where(sub == 1 + 2 * i + n, lane_gather(waves[n], pick), body)
-    msgs[0, SUBS : 2 * SUBS] = body
-
-    loads[1].wait()
-    flat = jnp.concatenate(
-        [sino_ref[i].astype(jnp.float32) for i in range(ang_dev)], axis=0
-    )
-    tiles = [flat[:, b * LANES : (b + 1) * LANES] for b in range(nblocks)]
+            rows = jnp.where(sub == 1 + 2 * i + n, lane_gather(waves[n], pick), rows)
+    msgs[0, SUBS : 2 * SUBS] = rows
+
     top = jnp.abs(tiles[0])
     for tile in tiles[1:]:
         top = jnp.maximum(top, jnp.abs(tile))
     top = jnp.broadcast_to(jnp.max(top, axis=1, keepdims=True), (SUBS, LANES))
     msgs[0, :SUBS] = jnp.maximum(top, 1e-30) * (0.51 / 32700)
 
-    split = []
-    for p in range(2):
-        index = (2 * lane + p) % LANES
-        picked = [lane_gather(tile, index) for tile in tiles]
-        split.append(
-            [
-                jnp.where(lane < LANES // 2, picked[2 * t], picked[2 * t + 1])
-                for t in range(nspans)
-            ]
-        )
-    lhs = [
-        jnp.concatenate(
-            [jnp.concatenate([part[2 * k], part[2 * k + 1]], axis=1) for k in range(kblocks)],
-            axis=0,
-        ).astype(jnp.bfloat16)
-        for part in split
-    ]
-    total = [
-        [split[1 - p][t] * 0.25 for t in range(nspans)] for p in range(2)
-    ]
+    def unzip(start):
+        picked = [lane_gather(tile, (2 * lane + start) % LANES) for tile in tiles]
+        at = 2 * lane + start
+        outs = []
+        for t in range(nspans):
+            out = jnp.where(at < LANES, picked[2 * t], picked[2 * t + 1])
+            if start < 0:
+                out = jnp.where(at < 0, picked[2 * t - 1] if t else 0.0, out)
+            outs.append(out)
+        return outs
+
+    evens, odds, late = unzip(0), unzip(1), unzip(-1)
+    lhs = jnp.concatenate(
+        [
+            jnp.concatenate([part[2 * k], part[2 * k + 1]], axis=1)
+            for part in (evens, late)
+            for k in range(kblocks)
+        ],
+        axis=0,
+    ).astype(jnp.bfloat16)
+    rest = jnp.broadcast_to(odds[-1][:, LANES - 1 :], (SUBS, LANES))
+    total = [[odds[t] * 0.25 for t in range(nspans)], [evens[t] * 0.25 for t in range(nspans)]]
     ready = 0
     for d in range(2 * kblocks - 1):
-        while cuts[ready] < 2 * d + 3:
+        while cuts[ready] < 2 * d + 4:
             weights[ready].wait()
             ready += 1
+        up = jnp.concatenate([slab[2 * d + 2], slab[2 * d + 3]], axis=1)
+        down = jnp.concatenate([slab[2 * d + 1], slab[2 * d + 2]], axis=1)
+        prod = jnp.dot(
+            lhs, jnp.concatenate([up, down], axis=0), preferred_element_type=jnp.float32
+        )
         for p in range(2):
-            up = jnp.concatenate([slab[2 * d + 1, p], slab[2 * d + 2, p]], axis=1)
-            down = jnp.concatenate([slab[2 * d, p], slab[2 * d + 1, p]], axis=1)
-            prod = jnp.dot(
-                lhs[p], jnp.concatenate([up, down], axis=0), preferred_element_type=jnp.float32
-            )
             for i in range(kblocks):
                 j = d - (kblocks - 1) + i
                 if 0 <= j < kblocks:
+                    row = (p * kblocks + i) * SUBS
                     for n in range(2):
                         total[p][2 * j + n] = (
                             total[p][2 * j + n]
-                            + prod[i * SUBS : (i + 1) * SUBS, n * LANES : (n + 1) * LANES]
+                            + prod[row : row + SUBS, n * LANES : (n + 1) * LANES]
                         )
+    for t in range(nspans):
+        ends_at = jnp.broadcast_to(slab[t, 0:1].astype(jnp.float32), (SUBS, LANES))
+        total[1][t] = total[1][t] + rest * ends_at
     for t in range(nspans):
         chunks[0, :, t * LANES : (t + 1) * LANES] = jnp.concatenate(
             [total[1][t], total[0][t]], axis=0
@@ -293,7 +296,7 @@
 
     pl.semaphore_wait(barrier, greeted)
 
-    for d in (3, 1, 2):
+    for d in SENDS:
         jplane(d).start()
 
     @pl.when(q == PLANE - 1)

time: 15.2 us -> 15 us (0.987)
  Pallas kernels: 14.4 us -> 14.2 us
    pallas_call x1, Pallas kernels: 14.4 us -> 14.2 us  [body(): pl.pallas_call(functools.partial(kernel, width), out_shape=pltpu.VMEM((ro...]
where the time goes in v5:
time: 15 us; the launch traced here: 14.8 us
  Pallas kernels  14.2 us (95%)
  local copies, waits for them, and re-layouts  0.63 us (4%)
    pallas_call x1, Pallas kernels, body(): pl.pallas_call(functools.partial(kernel, width), out_shape=pltpu.VMEM((ro...  14.2 us
    unnamed x1, local copies, waits for them, and re-layouts  0.63 us

profile of v5, /device:TPU:0, one launch (start us, length us, event | category | flops | bytes accessed | tf_op | source)
XLA Modules:
  0.0 14.8 jit_solution(4985755005627671246)
XLA Ops:
  0.0 14.2 %shard_map.55 = f32[2,4,2048]{2,1,0:T(4,128)S(1)} custom-call(bf16[1,2]{1,0:T(2,128)(2,1)} %bitcast.1, s32[32]{0:T(128)} %shift_hbm.1, bf16[2,4,2048]{2,1,0:T(4,128)(2,1)} %sino_hbm.1, bf16[16,128,128]{2,1,0:T(8,128)(2,1)} %constant.4.clone.slab_hbm, s32[16,1,128]{2,1,0:T(1,128)} %constant.5.clone.base_hbm), custom_call_target="tpu_custom_call" | custom-call | tf_op jit(solution)/shard_map/pallas_call | solution.py:526
  14.2 0.6 %copy.7 = f32[2,4,2048]{2,1,0:T(4,128)} copy(f32[2,4,2048]{2,1,0:T(4,128)S(1)} %shard_map.55) | data formatting | bytes 131072

commit v6 on v5

--- a/solution.py
+++ b/solution.py
@@ -16,9 +16,8 @@
 STEP = 64
 JITTER = 0.29882812
 SHIFT = 8
-PIECES = 1
-PARTS = 1
 SENDS = (1, 2, 3)
+GATHERS = [(i, p, s) for i in (0, 1) for p, s in ((0, 0), (1, 0), (1, 1), (0, 1))]
 MESH = pl.DeviceIdType.MESH
 
 
@@ -133,17 +132,8 @@
         )
     ]
     kblocks = bins // 2 // BLOCK
-    ntiles = slab.shape[0]
-    cuts = [0]
-    for piece in range(PIECES):
-        cuts.append(2 + 2 * -(-(2 * kblocks - 1) * (piece + 1) // PIECES))
-    weights = [
-        pltpu.make_async_copy(
-            slab_hbm.at[cuts[n] : cuts[n + 1]], slab.at[cuts[n] : cuts[n + 1]], wsem.at[n]
-        )
-        for n in range(PIECES)
-    ]
-    for load in loads[:2] + weights + loads[2:]:
+    weights = [pltpu.make_async_copy(slab_hbm, slab, wsem.at[0])]
+    for load in [loads[1], loads[0]] + weights + loads[2:]:
         load.start()
 
     barrier = pltpu.get_barrier_semaphore()
@@ -185,33 +175,33 @@
 
     def jnext(p):
         return remote(
-            jrow, msgs.at[PLANE, SUBS : 2 * SUBS], sj.at[PLANE - 1 + p], rj.at[PLANE - 1],
+            jrow, msgs.at[PLANE, SUBS : 2 * SUBS], lsem.at[p], rj.at[PLANE - 1],
             (z + 1) % depth * PLANE + p,
         )
 
     def jprev(p):
         return remote(
-            jrow, msgs.at[PLANE + 1, SUBS : 2 * SUBS], sj.at[PLANE - 1 + p], rj.at[PLANE],
+            jrow, msgs.at[PLANE + 1, SUBS : 2 * SUBS], lsem.at[p], rj.at[PLANE],
             (z - 1) * PLANE + p,
         )
 
     def jwrap():
         return remote(
             msgs.at[q, SUBS : 2 * SUBS], msgs.at[PLANE + 1, SUBS : 2 * SUBS],
-            sj.at[2 * PLANE - 1], rj.at[PLANE], (depth - 1) * PLANE + q,
+            wsem.at[0], rj.at[PLANE], (depth - 1) * PLANE + q,
         )
 
     def share(d):
         return remote(chunks.at[0], chunks.at[d], s1.at[d - 1], r1.at[d - 1], peer(d))
 
-    def give(zt, part):
+    def give(zt):
+        k = (zt - z + depth) % depth
+        return remote(snd.at[zt], rcv.at[k - 1], s2.at[k - 1], r2.at[k - 1], zt * PLANE + q)
+
+    def take(k):
         return remote(
-            snd.at[part, zt], rcv.at[part, z], s2.at[part, zt], r2.at[part, z], zt * PLANE + q
-        )
-
-    def take(zs, part):
-        return remote(
-            snd.at[part, zs], rcv.at[part, zs], s2.at[part, zs], r2.at[part, zs], zs * PLANE + q
+            snd.at[0], rcv.at[k - 1], s2.at[k - 1], r2.at[k - 1],
+            (z + depth - k) % depth * PLANE + q,
         )
 
     lane = lax.broadcasted_iota(jnp.int32, (SUBS, LANES), 1)
@@ -225,6 +215,27 @@
         [sino_ref[i].astype(jnp.float32) for i in range(ang_dev)], axis=0
     )
     tiles = [flat[:, b * LANES : (b + 1) * LANES] for b in range(nblocks)]
+    def unzip(start):
+        picked = [lane_gather(tile, (2 * lane + start) % LANES) for tile in tiles]
+        at = 2 * lane + start
+        outs = []
+        for t in range(nspans):
+            out = jnp.where(at < LANES, picked[2 * t], picked[2 * t + 1])
+            if start < 0:
+                out = jnp.where(at < 0, picked[2 * t - 1] if t else 0.0, out)
+            outs.append(out)
+        return outs
+
+    evens, odds, late = unzip(0), unzip(1), unzip(-1)
+    lhs = jnp.concatenate(
+        [
+            jnp.concatenate([part[2 * k], part[2 * k + 1]], axis=1)
+            for part in (evens, late)
+            for k in range(kblocks)
+        ],
+        axis=0,
+    ).astype(jnp.bfloat16)
+    weights[0].wait()
     mine = (lane % angles) - me * ang_dev
     msg = jnp.zeros((SUBS, LANES), jnp.float32)
     for i in range(ang_dev):
@@ -244,33 +255,9 @@
     top = jnp.broadcast_to(jnp.max(top, axis=1, keepdims=True), (SUBS, LANES))
     msgs[0, :SUBS] = jnp.maximum(top, 1e-30) * (0.51 / 32700)
 
-    def unzip(start):
-        picked = [lane_gather(tile, (2 * lane + start) % LANES) for tile in tiles]
-        at = 2 * lane + start
-        outs = []
-        for t in range(nspans):
-            out = jnp.where(at < LANES, picked[2 * t], picked[2 * t + 1])
-            if start < 0:
-                out = jnp.where(at < 0, picked[2 * t - 1] if t else 0.0, out)
-            outs.append(out)
-        return outs
-
-    evens, odds, late = unzip(0), unzip(1), unzip(-1)
-    lhs = jnp.concatenate(
-        [
-            jnp.concatenate([part[2 * k], part[2 * k + 1]], axis=1)
-            for part in (evens, late)
-            for k in range(kblocks)
-        ],
-        axis=0,
-    ).astype(jnp.bfloat16)
     rest = jnp.broadcast_to(odds[-1][:, LANES - 1 :], (SUBS, LANES))
     total = [[odds[t] * 0.25 for t in range(nspans)], [evens[t] * 0.25 for t in range(nspans)]]
-    ready = 0
     for d in range(2 * kblocks - 1):
-        while cuts[ready] < 2 * d + 4:
-            weights[ready].wait()
-            ready += 1
         up = jnp.concatenate([slab[2 * d + 2], slab[2 * d + 3]], axis=1)
         down = jnp.concatenate([slab[2 * d + 1], slab[2 * d + 2]], axis=1)
         prod = jnp.dot(
@@ -294,11 +281,21 @@
             [total[1][t], total[0][t]], axis=0
         ).astype(jnp.bfloat16)
 
+    loads[2].wait()
+    loads[3].wait()
     pl.semaphore_wait(barrier, greeted)
 
     for d in SENDS:
         jplane(d).start()
 
+    @pl.when((q == 0) & (z == 0))
+    def _():
+        jwrap().start()
+
+    for d in SENDS:
+        share(d).start()
+
+
     @pl.when(q == PLANE - 1)
     def _():
         for p in range(PLANE):
@@ -309,15 +306,6 @@
         for p in range(PLANE):
             jprev(p).start()
 
-    @pl.when((q == 0) & (z == 0))
-    def _():
-        jwrap().start()
-
-    for d in SENDS:
-        share(d).start()
-
-    loads[2].wait()
-    loads[3].wait()
 
     lead = sub % slices < slices // 2
     ypos = []
@@ -360,7 +348,8 @@
     def project(d, known, g, b):
         pc = peer(d)
         qc = pc - z * PLANE
-        sums = []
+        pairs = slices // 2
+        index, fracs, slots = [], [], []
         for i in range(ang_dev):
             cosb, parts, scales = known[i]
             moved = shift_ref[pc * ang_dev + i]
@@ -370,17 +359,21 @@
             h = cosb * (b * LANES - half) + parts[g] + offset
             odd = h.astype(jnp.int32)
             even = (h + 0.5).astype(jnp.int32)
-            frac = jnp.abs(h - even.astype(jnp.float32)) * 2.0
-            pairs = slices // 2
-            evens = [lane_gather(line(slot, i * slices + s), even) for s in range(pairs)]
-            odds = [lane_gather(line(slot, i * slices + pairs + s), odd) for s in range(pairs)]
+            fracs.append(jnp.abs(h - even.astype(jnp.float32)) * 2.0)
+            index.append((even, odd))
+            slots.append(slot)
+        words = {}
+        for i, p, s in GATHERS:
+            words[i, p, s] = lane_gather(line(slots[i], i * slices + p * pairs + s), index[i][p])
+        sums = []
+        for i in range(ang_dev):
             got = []
             for s in range(slices):
-                e, o = evens[s % pairs], odds[s % pairs]
+                e, o = words[i, 0, s % pairs], words[i, 1, s % pairs]
                 if s >= pairs:
                     e, o = lax.shift_left(e, 16), lax.shift_left(o, 16)
                 e, o = e.astype(jnp.float32), o.astype(jnp.float32)
-                got.append((e + frac * (o - e)) * scales[s])
+                got.append((e + fracs[i] * (o - e)) * known[i][2][s])
             sums.append(got)
         return sums
 
@@ -415,38 +408,37 @@
     def _():
         jplane(d).wait_recv()
 
-    jnext(0).wait_recv()
-    jprev(0).wait_recv()
-    share(d).wait_recv()
-    jit = sum(spoken(i, SUBS) for i in range(PLANE + 2))
-    ahead = pltpu.roll(jit, LANES - 1, 1)
-    behind = pltpu.roll(jit, 1, 1)
-    weight = (1.0 + (ahead - behind) * 1.5) * (4.0 / math.sqrt(angles))
-    weight = [
-        [
-            lane_gather(weight, jnp.full((SUBS, LANES), peer(n) * ang_dev + i, jnp.int32))
-            for i in range(ang_dev)
+    def weigh():
+        jnext(0).wait_recv()
+        jprev(0).wait_recv()
+        jit = sum(spoken(i, SUBS) for i in range(PLANE + 2))
+        ahead = pltpu.roll(jit, LANES - 1, 1)
+        behind = pltpu.roll(jit, 1, 1)
+        weight = (1.0 + (ahead - behind) * 1.5) * (4.0 / math.sqrt(angles))
+        return [
+            [
+                lane_gather(weight, jnp.full((SUBS, LANES), peer(n) * ang_dev + i, jnp.int32))
+                for i in range(ang_dev)
+            ]
+            for n in range(PLANE)
         ]
-        for n in range(PLANE)
-    ]
-    spread(d)
-    known = [angle(d, i) for i in range(ang_dev)]
+
+    def merge(weight, g, s, b, chunks_in):
+        terms = [
+            weight[n][i] * held[n, i, g, s, b] for n in chunks_in for i in range(ang_dev)
+        ]
+        while len(terms) > 1:
+            terms = [x + y for x, y in zip(terms[::2], terms[1::2])] + terms[len(terms) // 2 * 2 :]
+        return terms[0]
+
     pos = sub % zper
-    ntile = nblocks // 2 // PARTS
-    for part in range(PARTS):
-        for t in range(ntile):
+
+    def pack(rows_of):
+        for t in range(nblocks // 2):
             for g in range(groups):
                 out = [[], [], [], []]
-                for b in (2 * (part * ntile + t), 2 * (part * ntile + t) + 1):
-                    got = project(d, known, g, b)
-                    v = []
-                    for s in range(slices):
-                        terms = [weight[d][i] * got[i][s] for i in range(ang_dev)]
-                        for n in range(PLANE - 1):
-                            terms += [weight[n][i] * held[n, i, g, s, b] for i in range(ang_dev)]
-                        while len(terms) > 1:
-                            terms = [x + y for x, y in zip(terms[::2], terms[1::2])]
-                        v += terms
+                for b in (2 * t, 2 * t + 1):
+                    v = rows_of(g, b)
                     w = [None] * 4
                     for s in range(2):
                         w[s] = jnp.where(pos < 2, v[s], pltpu.roll(v[s + 2], 2, 0))
@@ -458,38 +450,50 @@
                             fin[g * zper + n, b] = val
                             out[n].append(val)
                 for n in range(4):
-                    snd[part, g * zper + n, :, t * LANES : (t + 1) * LANES] = jnp.concatenate(
+                    snd[g * zper + n, :, t * LANES : (t + 1) * LANES] = jnp.concatenate(
                         out[n], axis=0
                     ).astype(jnp.bfloat16)
 
-        @pl.loop(0, depth)
-        def _(zt):
-            @pl.when(zt != z)
-            def _():
-                give(zt, part).start()
-
-    for part in range(PARTS):
-        @pl.loop(1, depth)
-        def _(k):
-            take((z + k) % depth, part).wait_recv()
-
-        for t in range(ntile):
-            b = 2 * (part * ntile + t)
-            sums = [fin[z, b], fin[z, b + 1]]
-            for k in range(1, depth):
-                both = rcv[part, (z + k) % depth, :, t * LANES : (t + 1) * LANES]
-                both = both.astype(jnp.float32)
-                sums = [sums[0] + both[:SUBS], sums[1] + both[SUBS:]]
-            for j in range(2):
-                cols = slice((b + j) * LANES, (b + j + 1) * LANES)
-                for r in range(rows_dev):
-                    out_ref[r, :, cols] = sums[j][r * slices : (r + 1) * slices]
-
-    for d in range(1, PLANE):
-        jplane(d).wait_send()
-        share(d).wait_send()
-
-    @pl.when(q == PLANE - 1)
+    waits_last = (z == depth - 1) & (q > 0)
+
+    @pl.when(waits_last)
+    def _():
+        share(d).wait_recv()
+        keep(d)
+        weight = weigh()
+        pack(lambda g, b: [merge(weight, g, s, b, range(PLANE)) for s in range(slices)])
+
+    @pl.when(jnp.logical_not(waits_last))
+    def _():
+        weight = weigh()
+        for b in range(nblocks):
+            for g in range(groups):
+                for s in range(slices):
+                    held[0, 0, g, s, b] = merge(weight, g, s, b, range(PLANE - 1))
+        share(d).wait_recv()
+        spread(d)
+        known = [angle(d, i) for i in range(ang_dev)]
+
+        def rows_of(g, b):
+            got = project(d, known, g, b)
+            return [
+                held[0, 0, g, s, b] + (weight[d][0] * got[0][s] + weight[d][1] * got[1][s])
+                for s in range(slices)
+            ]
+
+        pack(rows_of)
+
+    for n in range(1, PLANE):
+        jplane(n).wait_send()
+        share(n).wait_send()
+
+    @pl.loop(0, depth)
+    def _(zt):
+        @pl.when(zt != z)
+        def _():
+            give(zt).start()
+
+    @pl.when(q == ends)
     def _():
         for p in range(PLANE):
             jnext(p).wait_send()
@@ -503,10 +507,23 @@
     def _():
         jwrap().wait_send()
 
-    for part in range(PARTS):
-        @pl.loop(1, depth)
-        def _(k):
-            give((z + k) % depth, part).wait_send()
+    @pl.loop(1, depth)
+    def _(k):
+        take(k).wait_recv()
+
+    for t in range(nblocks // 2):
+        sums = [fin[z, 2 * t], fin[z, 2 * t + 1]]
+        for k in range(1, depth):
+            both = rcv[k - 1, :, t * LANES : (t + 1) * LANES].astype(jnp.float32)
+            sums = [sums[0] + both[:SUBS], sums[1] + both[SUBS:]]
+        for j in range(2):
+            cols = slice((2 * t + j) * LANES, (2 * t + j + 1) * LANES)
+            for r in range(rows_dev):
+                out_ref[r, :, cols] = sums[j][r * slices : (r + 1) * slices]
+
+    @pl.loop(1, depth)
+    def _(k):
+        give((z + k) % depth).wait_send()
 
 
 def body(sinogram, jitter, shift):
@@ -537,18 +554,18 @@
             pltpu.VMEM((PLANE, 2 * SUBS, bins // 2), jnp.bfloat16),
             pltpu.VMEM((PLANE + 2, 2 * SUBS, LANES), jnp.float32),
             pltpu.VMEM((bins // STEP + 2, SUBS, LANES), jnp.int32),
-            pltpu.VMEM((PLANE - 1, ang_dev, groups, slices, nblocks, SUBS, LANES), jnp.float32),
+            pltpu.VMEM((PLANE, ang_dev, groups, slices, nblocks, SUBS, LANES), jnp.float32),
             pltpu.VMEM((depth, nblocks, SUBS, LANES), jnp.float32),
-            pltpu.VMEM((PARTS, depth, 2 * SUBS, bins // 2 // PARTS), jnp.bfloat16),
-            pltpu.VMEM((PARTS, depth, 2 * SUBS, bins // 2 // PARTS), jnp.bfloat16),
+            pltpu.VMEM((depth, 2 * SUBS, bins // 2), jnp.bfloat16),
+            pltpu.VMEM((depth - 1, 2 * SUBS, bins // 2), jnp.bfloat16),
             dma((4,)),
-            dma((PIECES,)),
-            dma((2 * PLANE,)),
+            dma((1,)),
+            dma((PLANE - 1,)),
             dma((PLANE + 1,)),
             dma((PLANE - 1,)),
             dma((PLANE - 1,)),
-            dma((PARTS, depth)),
-            dma((PARTS, depth)),
+            dma((depth - 1,)),
+            dma((depth - 1,)),
         ],
         compiler_params=pltpu.CompilerParams(collective_id=0, has_side_effects=True),
     )(jitter.reshape(1, ang_dev), shift, sinogram, slab, base)

time: 15 us -> 15 us (level)
  no operation moved by 1% of the time
where the time goes in v6:
time: 15 us; the launch traced here: 14.9 us
  Pallas kernels  14.3 us (95%)
  local copies, waits for them, and re-layouts  0.63 us (4%)
    pallas_call x1, Pallas kernels, body(): pl.pallas_call(functools.partial(kernel, width), out_shape=pltpu.VMEM((ro...  14.3 us
    unnamed x1, local copies, waits for them, and re-layouts  0.63 us

profile of v6, /device:TPU:0, one launch (start us, length us, event | category | flops | bytes accessed | tf_op | source)
XLA Modules:
  0.0 14.9 jit_solution(5409691712299276845)
XLA Ops:
  0.0 14.3 %shard_map.55 = f32[2,4,2048]{2,1,0:T(4,128)S(1)} custom-call(bf16[1,2]{1,0:T(2,128)(2,1)} %bitcast.1, s32[32]{0:T(128)} %shift_hbm.1, bf16[2,4,2048]{2,1,0:T(4,128)(2,1)} %sino_hbm.1, bf16[16,128,128]{2,1,0:T(8,128)(2,1)} %constant.4.clone.slab_hbm, s32[16,1,128]{2,1,0:T(1,128)} %constant.5.clone.base_hbm), custom_call_target="tpu_custom_call" | custom-call | tf_op jit(solution)/shard_map/pallas_call | solution.py:543
  14.3 0.6 %copy.7 = f32[2,4,2048]{2,1,0:T(4,128)} copy(f32[2,4,2048]{2,1,0:T(4,128)S(1)} %shard_map.55) | data formatting | bytes 131072

commit v7 on v6

--- a/solution.py
+++ b/solution.py
@@ -16,7 +16,7 @@
 STEP = 64
 JITTER = 0.29882812
 SHIFT = 8
-SENDS = (1, 2, 3)
+SENDS = (1, 3, 2)
 GATHERS = [(i, p, s) for i in (0, 1) for p, s in ((0, 0), (1, 0), (1, 1), (0, 1))]
 MESH = pl.DeviceIdType.MESH
 
@@ -83,7 +83,7 @@
     base,
     chunks,
     msgs,
-    tab,
+    both_tabs,
     held,
     fin,
     snd,
@@ -168,26 +168,26 @@
         + ends * ((PLANE - 1 - q) // ends) * ((z + depth - 1) // depth)
     )
 
-    jrow = msgs.at[0, SUBS : 2 * SUBS]
+    jrow = msgs.at[0, 0]
 
     def jplane(d):
         return remote(msgs.at[0], msgs.at[d], sj.at[d - 1], rj.at[d - 1], peer(d))
 
     def jnext(p):
         return remote(
-            jrow, msgs.at[PLANE, SUBS : 2 * SUBS], lsem.at[p], rj.at[PLANE - 1],
+            jrow, msgs.at[PLANE, 0], lsem.at[p], rj.at[PLANE - 1],
             (z + 1) % depth * PLANE + p,
         )
 
     def jprev(p):
         return remote(
-            jrow, msgs.at[PLANE + 1, SUBS : 2 * SUBS], lsem.at[p], rj.at[PLANE],
+            jrow, msgs.at[PLANE + 1, 0], lsem.at[p], rj.at[PLANE],
             (z - 1) * PLANE + p,
         )
 
     def jwrap():
         return remote(
-            msgs.at[q, SUBS : 2 * SUBS], msgs.at[PLANE + 1, SUBS : 2 * SUBS],
+            msgs.at[q, 0], msgs.at[PLANE + 1, 0],
             wsem.at[0], rj.at[PLANE], (depth - 1) * PLANE + q,
         )
 
@@ -207,7 +207,9 @@
     lane = lax.broadcasted_iota(jnp.int32, (SUBS, LANES), 1)
     sub = lax.broadcasted_iota(jnp.int32, (SUBS, LANES), 0)
     lanef = lane.astype(jnp.float32)
-    tab[tab.shape[0] - 1] = jnp.zeros((SUBS, LANES), jnp.int32)
+    tabs = [both_tabs.at[n] for n in range(both_tabs.shape[0])]
+    for tab in tabs:
+        tab[tab.shape[0] - 1] = jnp.zeros((SUBS, LANES), jnp.int32)
 
     loads[0].wait()
     loads[1].wait()
@@ -242,18 +244,19 @@
         msg = jnp.where(mine == i, jit_ref[0:1, i : i + 1].astype(jnp.float32), msg)
     theta = ((lane % angles).astype(jnp.float32) + msg) * math.pi / angles
     waves = [jnp.cos(theta) * 0.5, jnp.sin(theta) * 0.5]
-    rows = msg
+    facts = jnp.zeros((SUBS, LANES), jnp.float32)
     for i in range(ang_dev):
         pick = jnp.full((SUBS, LANES), me * ang_dev + i, jnp.int32)
         for n in range(2):
-            rows = jnp.where(sub == 1 + 2 * i + n, lane_gather(waves[n], pick), rows)
-    msgs[0, SUBS : 2 * SUBS] = rows
-
+            facts = jnp.where(lane == SUBS + 2 * i + n, lane_gather(waves[n], pick), facts)
     top = jnp.abs(tiles[0])
     for tile in tiles[1:]:
         top = jnp.maximum(top, jnp.abs(tile))
     top = jnp.broadcast_to(jnp.max(top, axis=1, keepdims=True), (SUBS, LANES))
-    msgs[0, :SUBS] = jnp.maximum(top, 1e-30) * (0.51 / 32700)
+    scale = jnp.maximum(top, 1e-30) * (0.51 / 32700)
+    scale = jnp.sum(jnp.where(lane == sub, scale, 0.0), axis=0, keepdims=True)
+    msgs[0, 0] = msg[:1]
+    msgs[0, 1] = scale + facts[:1]
 
     rest = jnp.broadcast_to(odds[-1][:, LANES - 1 :], (SUBS, LANES))
     total = [[odds[t] * 0.25 for t in range(nspans)], [evens[t] * 0.25 for t in range(nspans)]]
@@ -313,8 +316,10 @@
         row = ((sub % zper + g * zper) * PLANE + q) * rows_dev + sub // zper
         ypos.append(row.astype(jnp.float32) - (nrows - 1) / 2)
 
-    def spread(d):
-        inverse = 1.0 / msgs[d, :SUBS]
+    def heard(d, row):
+        return jnp.broadcast_to(msgs[d, row], (SUBS, LANES))
+
+    def spread(d, inverse, tab):
         words = []
         for t in range(nspans):
             both = chunks[d, :, t * LANES : (t + 1) * LANES].astype(jnp.float32)
@@ -333,19 +338,25 @@
             if j == 3:
                 tab[0] = jnp.where(lane < cut, 0, turned[0])
 
-    def spoken(d, row):
-        return jnp.broadcast_to(msgs[d, row : row + 1], (SUBS, LANES))
-
-    def angle(d, i):
-        cosb, sinb = (spoken(d, SUBS + 1 + 2 * i + n) for n in range(2))
-        parts = [lanef * cosb + ypos[g] * sinb for g in range(groups)]
-        scales = [spoken(d, i * slices + s) * (1.0 / 65536) for s in range(slices)]
-        return cosb, parts, scales
-
-    def line(slot, row):
+    def learn(d):
+        facts = heard(d, 1)
+
+        def fact(n):
+            return lane_gather(facts, jnp.full((SUBS, LANES), n, jnp.int32))
+
+        known = []
+        for i in range(ang_dev):
+            cosb, sinb = (fact(SUBS + 2 * i + n) for n in range(2))
+            parts = [lanef * cosb + ypos[g] * sinb for g in range(groups)]
+            known.append(
+                (cosb, parts, [fact(i * slices + s) * (1.0 / 65536) for s in range(slices)])
+            )
+        return known, 1.0 / lane_gather(facts, sub)
+
+    def line(tab, slot, row):
         return jnp.broadcast_to(tab[slot, row : row + 1], (SUBS, LANES))
 
-    def project(d, known, g, b):
+    def project(d, known, tab, g, b):
         pc = peer(d)
         qc = pc - z * PLANE
         pairs = slices // 2
@@ -364,7 +375,7 @@
             slots.append(slot)
         words = {}
         for i, p, s in GATHERS:
-            words[i, p, s] = lane_gather(line(slots[i], i * slices + p * pairs + s), index[i][p])
+            words[i, p, s] = lane_gather(line(tab, slots[i], i * slices + p * pairs + s), index[i][p])
         sums = []
         for i in range(ang_dev):
             got = []
@@ -377,14 +388,19 @@
             sums.append(got)
         return sums
 
-    def keep(d):
-        spread(d)
-        known = [angle(d, i) for i in range(ang_dev)]
+    def keep(*group):
+        learnt = [learn(d) for d in group]
+        for d in group:
+            if d > 0:
+                share(d).wait_recv()
+        for d, tab, (_, inverse) in zip(group, tabs, learnt):
+            spread(d, inverse, tab)
         for b in range(nblocks):
             for g in range(groups):
-                for i, got in enumerate(project(d, known, g, b)):
-                    for s in range(slices):
-                        held[d, i, g, s, b] = got[s]
+                for d, tab, (known, _) in zip(group, tabs, learnt):
+                    for i, got in enumerate(project(d, known, tab, g, b)):
+                        for s in range(slices):
+                            held[d, i, g, s, b] = got[s]
 
     keep(0)
 
@@ -393,25 +409,21 @@
         jplane(q).wait_recv()
         jwrap().start()
 
-    @pl.loop(1, PLANE - 1)
-    def _(d):
+    def meet(d):
         @pl.when((z > 0) | (q != d))
         def _():
             jplane(d).wait_recv()
 
-        share(d).wait_recv()
-        keep(d)
-
+    for d in range(1, PLANE - 1):
+        meet(d)
+    keep(*range(1, PLANE - 1))
     d = PLANE - 1
-
-    @pl.when((z > 0) | (q != d))
-    def _():
-        jplane(d).wait_recv()
+    meet(d)
 
     def weigh():
         jnext(0).wait_recv()
         jprev(0).wait_recv()
-        jit = sum(spoken(i, SUBS) for i in range(PLANE + 2))
+        jit = sum(heard(i, 0) for i in range(PLANE + 2))
         ahead = pltpu.roll(jit, LANES - 1, 1)
         behind = pltpu.roll(jit, 1, 1)
         weight = (1.0 + (ahead - behind) * 1.5) * (4.0 / math.sqrt(angles))
@@ -458,7 +470,6 @@
 
     @pl.when(waits_last)
     def _():
-        share(d).wait_recv()
         keep(d)
         weight = weigh()
         pack(lambda g, b: [merge(weight, g, s, b, range(PLANE)) for s in range(slices)])
@@ -466,18 +477,15 @@
     @pl.when(jnp.logical_not(waits_last))
     def _():
         weight = weigh()
-        for b in range(nblocks):
-            for g in range(groups):
-                for s in range(slices):
-                    held[0, 0, g, s, b] = merge(weight, g, s, b, range(PLANE - 1))
+        known, inverse = learn(d)
         share(d).wait_recv()
-        spread(d)
-        known = [angle(d, i) for i in range(ang_dev)]
+        spread(d, inverse, tabs[0])
 
         def rows_of(g, b):
-            got = project(d, known, g, b)
+            got = project(d, known, tabs[0], g, b)
             return [
-                held[0, 0, g, s, b] + (weight[d][0] * got[0][s] + weight[d][1] * got[1][s])
+                merge(weight, g, s, b, range(PLANE - 1))
+                + (weight[d][0] * got[0][s] + weight[d][1] * got[1][s])
                 for s in range(slices)
             ]
 
@@ -552,8 +560,8 @@
             pltpu.VMEM(slab.shape, jnp.bfloat16),
             pltpu.SMEM(base.shape[1:], jnp.int32),
             pltpu.VMEM((PLANE, 2 * SUBS, bins // 2), jnp.bfloat16),
-            pltpu.VMEM((PLANE + 2, 2 * SUBS, LANES), jnp.float32),
-            pltpu.VMEM((bins // STEP + 2, SUBS, LANES), jnp.int32),
+            pltpu.VMEM((PLANE + 2, 2, 1, LANES), jnp.float32),
+            pltpu.VMEM((PLANE - 2, bins // STEP + 2, SUBS, LANES), jnp.int32),
             pltpu.VMEM((PLANE, ang_dev, groups, slices, nblocks, SUBS, LANES), jnp.float32),
             pltpu.VMEM((depth, nblocks, SUBS, LANES), jnp.float32),
             pltpu.VMEM((depth, 2 * SUBS, bins // 2), jnp.bfloat16),

time: 15 us -> 14.9 us (level)
  Pallas kernels: 14.3 us -> 14.1 us
where the time goes in v7:
time: 14.9 us; the launch traced here: 14.8 us
  Pallas kernels  14.1 us (95%)
  local copies, waits for them, and re-layouts  0.63 us (4%)
    pallas_call x1, Pallas kernels, body(): pl.pallas_call(functools.partial(kernel, width), out_shape=pltpu.VMEM((ro...  14.1 us
    unnamed x1, local copies, waits for them, and re-layouts  0.63 us

profile of v7, /device:TPU:0, one launch (start us, length us, event | category | flops | bytes accessed | tf_op | source)
XLA Modules:
  0.0 14.8 jit_solution(14110240511369152679)
XLA Ops:
  0.0 14.1 %shard_map.55 = f32[2,4,2048]{2,1,0:T(4,128)S(1)} custom-call(bf16[1,2]{1,0:T(2,128)(2,1)} %bitcast.1, s32[32]{0:T(128)} %shift_hbm.1, bf16[2,4,2048]{2,1,0:T(4,128)(2,1)} %sino_hbm.1, bf16[16,128,128]{2,1,0:T(8,128)(2,1)} %constant.4.clone.slab_hbm, s32[16,1,128]{2,1,0:T(1,128)} %constant.5.clone.base_hbm), custom_call_target="tpu_custom_call" | custom-call | tf_op jit(solution)/shard_map/pallas_call | solution.py:551
  14.1 0.6 %copy.7 = f32[2,4,2048]{2,1,0:T(4,128)} copy(f32[2,4,2048]{2,1,0:T(4,128)S(1)} %shard_map.55) | data formatting | bytes 131072

commit v8 on v7

--- a/solution.py
+++ b/solution.py
@@ -16,7 +16,7 @@
 STEP = 64
 JITTER = 0.29882812
 SHIFT = 8
-SENDS = (1, 3, 2)
+SENDS = ((1, 2, 3), (2, 1, 3))
 GATHERS = [(i, p, s) for i in (0, 1) for p, s in ((0, 0), (1, 0), (1, 1), (0, 1))]
 MESH = pl.DeviceIdType.MESH
 
@@ -288,15 +288,18 @@
     loads[3].wait()
     pl.semaphore_wait(barrier, greeted)
 
-    for d in SENDS:
+    for d in SENDS[0]:
         jplane(d).start()
 
     @pl.when((q == 0) & (z == 0))
     def _():
         jwrap().start()
 
-    for d in SENDS:
-        share(d).start()
+    for side, order in enumerate(SENDS):
+        @pl.when(lax.axis_index("slab") % 2 == side)
+        def _():
+            for d in order:
+                share(d).start()
 
 
     @pl.when(q == PLANE - 1)
@@ -491,15 +494,15 @@
 
         pack(rows_of)
 
-    for n in range(1, PLANE):
-        jplane(n).wait_send()
-        share(n).wait_send()
-
     @pl.loop(0, depth)
     def _(zt):
         @pl.when(zt != z)
         def _():
             give(zt).start()
+
+    for n in range(1, PLANE):
+        jplane(n).wait_send()
+        share(n).wait_send()
 
     @pl.when(q == ends)
     def _():

time: 14.9 us -> 14.9 us (level)
  no operation moved by 1% of the time
where the time goes in v8:
time: 14.9 us; the launch traced here: 14.8 us
  Pallas kernels  14.1 us (95%)
  local copies, waits for them, and re-layouts  0.63 us (4%)
    pallas_call x1, Pallas kernels, body(): pl.pallas_call(functools.partial(kernel, width), out_shape=pltpu.VMEM((ro...  14.1 us
    unnamed x1, local copies, waits for them, and re-layouts  0.63 us

profile of v8, /device:TPU:0, one launch (start us, length us, event | category | flops | bytes accessed | tf_op | source)
XLA Modules:
  0.0 14.8 jit_solution(18350374574990001572)
XLA Ops:
  0.0 14.1 %shard_map.55 = f32[2,4,2048]{2,1,0:T(4,128)S(1)} custom-call(bf16[1,2]{1,0:T(2,128)(2,1)} %bitcast.1, s32[32]{0:T(128)} %shift_hbm.1, bf16[2,4,2048]{2,1,0:T(4,128)(2,1)} %sino_hbm.1, bf16[16,128,128]{2,1,0:T(8,128)(2,1)} %constant.4.clone.slab_hbm, s32[16,1,128]{2,1,0:T(1,128)} %constant.5.clone.base_hbm), custom_call_target="tpu_custom_call" | custom-call | tf_op jit(solution)/shard_map/pallas_call | solution.py:554
  14.1 0.6 %copy.7 = f32[2,4,2048]{2,1,0:T(4,128)} copy(f32[2,4,2048]{2,1,0:T(4,128)S(1)} %shard_map.55) | data formatting | bytes 131072

commit v9 on v8

--- a/solution.py
+++ b/solution.py
@@ -133,7 +133,7 @@
     ]
     kblocks = bins // 2 // BLOCK
     weights = [pltpu.make_async_copy(slab_hbm, slab, wsem.at[0])]
-    for load in [loads[1], loads[0]] + weights + loads[2:]:
+    for load in [loads[1], loads[0]] + weights:
         load.start()
 
     barrier = pltpu.get_barrier_semaphore()
@@ -161,6 +161,9 @@
     @pl.when((q != 0) & (z < depth - 1))
     def _():
         hello((z + 1) * PLANE)
+
+    for load in loads[2:]:
+        load.start()
 
     greeted = (
         ends + depth - 1

time: 14.9 us -> 14.9 us (level)
  no operation moved by 1% of the time
where the time goes in v9:
time: 14.9 us; the launch traced here: 14.8 us
  Pallas kernels  14.1 us (95%)
  local copies, waits for them, and re-layouts  0.63 us (4%)
    pallas_call x1, Pallas kernels, body(): pl.pallas_call(functools.partial(kernel, width), out_shape=pltpu.VMEM((ro...  14.1 us
    unnamed x1, local copies, waits for them, and re-layouts  0.63 us

profile of v9, /device:TPU:0, one launch (start us, length us, event | category | flops | bytes accessed | tf_op | source)
XLA Modules:
  0.0 14.8 jit_solution(6160548995110463643)
XLA Ops:
  0.0 14.1 %shard_map.55 = f32[2,4,2048]{2,1,0:T(4,128)S(1)} custom-call(bf16[1,2]{1,0:T(2,128)(2,1)} %bitcast.1, s32[32]{0:T(128)} %shift_hbm.1, bf16[2,4,2048]{2,1,0:T(4,128)(2,1)} %sino_hbm.1, bf16[16,128,128]{2,1,0:T(8,128)(2,1)} %constant.4.clone.slab_hbm, s32[16,1,128]{2,1,0:T(1,128)} %constant.5.clone.base_hbm), custom_call_target="tpu_custom_call" | custom-call | tf_op jit(solution)/shard_map/pallas_call | solution.py:557
  14.1 0.6 %copy.7 = f32[2,4,2048]{2,1,0:T(4,128)} copy(f32[2,4,2048]{2,1,0:T(4,128)S(1)} %shard_map.55) | data formatting | bytes 131072
